TPU v7x, 32 devices: a whole 2x2x4 slice. The times are simulated.
32 devices in a mesh: gx: 2 (over x), gy: 4 (over y, core), gz: 4 (over z).
Axes of the slice: x: 2, y: 2, z: 4, core: 2. Of those that a mesh axis runs over, the one named last changes fastest.
Arguments:
- velocity: float32 [3, 32, 64, 1024], P(None, 'gx', 'gy', 'gz'), may hold values from -24 to 24
- metric: float32 [3, 32, 64, 1024], P(None, 'gx', 'gy', 'gz'), may hold values from 0.5 to 2
Outputs:
- viscosity: float32 [32, 64, 1024], P('gx', 'gy', 'gz')
- coefficient: float32 [32, 64], P('gx', 'gy')
All inputs are finite; a program needn't handle non-finite values.
Results may differ from a plain program's by a relative error of at most 0.0003.
Values sent between devices are 32-bit elements; how exact they have to be, the bound alone decides.
A program may use at most 64 MiB of HBM per device.

v0:
```python
import functools

import jax
import jax.numpy as jnp
from jax import lax
from jax.experimental import pallas as pl
from jax.experimental.pallas import tpu as pltpu
from jax.sharding import PartitionSpec as P

MESH = pl.DeviceIdType.MESH
pairs = ((0, 0), (1, 1), (2, 2), (0, 1), (0, 2), (1, 2))
pair_weight = (1.0, 1.0, 1.0, 2.0, 2.0, 2.0)
eps_line = 1e-06
offsets = [(dx, dy, dz) for dz in (1, -1, 0) for dx in (0, 1, -1) for dy in (0, 1, -1) if (dx, dy, dz) != (0, 0, 0)]


def edge_slots(nx):
    ends = [0, 1, nx - 2, nx - 1]
    order = [(f, x) for f in range(6) for x in ends] + [(f, x) for f in range(6) for x in range(2, nx - 2)]
    return {key: 2 * n for n, key in enumerate(order)}


def kernel(sizes, vel, met, d_out, coef_out, D, V, Gv, G, H, Q, F, PK, R, LS, PS, sem_in, send, recv, lsend, lrecv, psend, precv):
    NX, NY, NZ = sizes
    nx, ny, nz = vel.shape[1:]
    yr, zr = ny + 8, nz + 128
    slots = edge_slots(nx)
    lanes_packed = PK.shape[2]
    ix, iy, iz = lax.axis_index("gx"), lax.axis_index("gy"), lax.axis_index("gz")

    load_v = pltpu.make_async_copy(vel, V.at[0:3, 2 : 2 + nx, 0:ny, 0:nz], sem_in.at[0])
    load_m = pltpu.make_async_copy(met, V.at[3:6, 2 : 2 + nx, 0:ny, 0:nz], sem_in.at[1])
    load_v.start()
    load_m.start()

    def exists(d):
        ok = None
        for delta, i, n in ((d[0], ix, NX), (d[1], iy, NY)):
            if delta:
                c = (i + delta >= 0) & (i + delta < n)
                ok = c if ok is None else ok & c
        return ok

    def when(cond, fn):
        if cond is None:
            fn()
        else:
            pl.when(cond)(fn)

    def dev(d):
        return (ix + d[0], iy + d[1], lax.rem(iz + d[2] + NZ, NZ))

    zplane = jnp.zeros((yr, zr), jnp.float32)
    for f in range(6):
        for xi in (0, 1, nx + 2, nx + 3):
            V[f, xi] = zplane
        def clear(x, _, f=f):
            V[f, x, ny:yr, :] = zplane[0:8]
            return 0
        lax.fori_loop(2, 2 + nx, clear, 0)
    for s in range(2):
        for dx in range(3):
            for dy in range(3):
                R[s, dx, dy] = jnp.zeros((ny, lanes_packed), jnp.float32)

    barrier = pltpu.get_barrier_semaphore()
    expected = jnp.int32(0)
    for d in offsets:
        ok = exists(d)
        def sig(d=d):
            pl.semaphore_signal(barrier, inc=1, device_id=dev(d), device_id_type=MESH)
        when(ok, sig)
        expected = expected + (1 if ok is None else ok.astype(jnp.int32))
    for o in range(1, NZ):
        pl.semaphore_signal(barrier, inc=1, device_id=(ix, iy, lax.rem(iz + o, NZ)), device_id_type=MESH)
    plane_peers = [(a, b) for a in range(NX) for b in range(NY) if (a, b) != (0, 0)]
    for a, b in plane_peers:
        pl.semaphore_signal(barrier, inc=1, device_id=(lax.rem(ix + a, NX), lax.rem(iy + b, NY), iz), device_id_type=MESH)
    expected = expected + (NZ - 1 + len(plane_peers))

    load_v.wait()
    load_m.wait()

    lane = lax.broadcasted_iota(jnp.int32, (ny, 128), 1)
    half = lane // 2
    acc = [[jnp.zeros((ny, 128), jnp.float32) for _ in range(lanes_packed // 128)] for _ in range(2)]
    for (f, x), p in slots.items():
        t, l = divmod(p, 128)
        here = half == l // 2
        hi = V[f, x + 2, 0:ny, nz - 128 : nz]
        lo = V[f, x + 2, 0:ny, 0:128]
        s_hi, s_lo = (l - 126) % 128, l
        acc[0][t] = jnp.where(here, pltpu.roll(hi, s_hi, 1) if s_hi else hi, acc[0][t])
        acc[1][t] = jnp.where(here, pltpu.roll(lo, s_lo, 1) if s_lo else lo, acc[1][t])
    for s in range(2):
        for t in range(lanes_packed // 128):
            PK[s, :, 128 * t : 128 * t + 128] = acc[s][t]

    pl.semaphore_wait(barrier, expected)

    def span_x(dx, metric):
        if dx == 0:
            return (2, 2, nx)
        if dx == 1:
            return (nx + 1, 1, 1) if metric else (nx, 0, 2)
        return (2, nx + 2, 1) if metric else (2, nx + 2, 2)

    def span_y(dy, metric):
        if dy == 0:
            return (0, 0, ny)
        if dy == 1:
            return (ny - 1, ny + 7, 1) if metric else (ny - 2, ny + 6, 2)
        return (0, ny, 1) if metric else (0, ny, 2)

    def copies(n, d):
        dx, dy, dz = d
        out = []
        if dz:
            s = 0 if dz == 1 else 1
            r0, rn = (0, ny) if dy == 0 else ((ny - 8, 8) if dy == 1 else (0, 8))
            ln = lanes_packed if dx == 0 else 128
            out.append((PK.at[s, r0 : r0 + rn, 0:ln], R.at[s, dx + 1, dy + 1, r0 : r0 + rn, 0:ln], 2 * n))
        else:
            for k in range(2):
                xs, xd, xn = span_x(dx, k == 1)
                ys, yd, yn = span_y(dy, k == 1)
                f0 = 3 * k
                out.append((
                    V.at[f0 : f0 + 3, xs : xs + xn, ys : ys + yn, 0:nz],
                    V.at[f0 : f0 + 3, xd : xd + xn, yd : yd + yn, 0:nz],
                    2 * n + k,
                ))
        return [
            pltpu.make_async_remote_copy(src_ref=a, dst_ref=b, send_sem=send.at[j], recv_sem=recv.at[j], device_id=dev(d), device_id_type=MESH)
            for a, b, j in out
        ]

    for n, d in enumerate(offsets):
        def go(n=n, d=d):
            for c in copies(n, d):
                c.start()
        when(exists(d), go)
    def land(wanted):
        for n, d in enumerate(offsets):
            if wanted(d):
                def arrive(n=n, d=d):
                    for c in copies(n, d):
                        c.wait_recv()
                when(exists((-d[0], -d[1], -d[2])), arrive)

    land(lambda d: d[0] == 0 and d[2] != 0)

    lane_r = lax.broadcasted_iota(jnp.int32, (yr, 128), 1)
    low_rows = lax.broadcasted_iota(jnp.int32, (8, 128), 0) < 4
    def packed(s, dx, t):
        cut = slice(128 * t, 128 * t + 128)
        edge = jnp.where(low_rows, R[s, dx, 0, 0:8, cut], R[s, dx, 2, ny - 8 : ny, cut])
        return jnp.concatenate([R[s, dx, 1, :, cut], edge], axis=0)
    tiles = {}
    def fill_span(f, planes):
        for xi in planes:
            if f >= 3 and xi in (0, nx + 3):
                continue
            if xi < 2:
                dx, x = 2, nx - 2 + xi
            elif xi >= nx + 2:
                dx, x = 0, xi - nx - 2
            else:
                dx, x = 1, xi - 2
            t, l = divmod(slots[(f, x)], 128)
            for s in range(2):
                if (s, dx, t) not in tiles:
                    tiles[(s, dx, t)] = packed(s, dx, t)
            a = pltpu.roll(tiles[(0, dx, t)], (126 - l) % 128, 1) if l != 126 else tiles[(0, dx, t)]
            b = pltpu.roll(tiles[(1, dx, t)], (128 - l) % 128, 1) if l else tiles[(1, dx, t)]
            V[f, xi, :, nz:zr] = jnp.where(lane_r < 64, b, a)

    for f in range(6):
        fill_span(f, range(2, nx + 2))
    land(lambda d: d[0] == 0 and d[2] == 0)

    def up(a, axis):
        return pltpu.roll(a, a.shape[axis] - 1, axis)

    def down(a, axis):
        return pltpu.roll(a, 1, axis)

    def smooth(a, axis):
        if axis == 1:
            return (a + a) + (up(a, 1) + down(a, 1))
        t = a + down(a, axis)
        return t + up(t, axis)

    def velocity_plane(x, _):
        for c in range(3):
            Gv[c, x] = smooth(smooth(V[c, x], 0), 1)
        return 0


    def strains(load, m, x):
        d = [[None] * 3 for _ in range(3)]
        for i in range(3):
            here = load(i, x)
            d[i][0] = m[0] * (load(i, x + 1) - load(i, x - 1))
            d[i][1] = m[1] * (up(here, 0) - down(here, 0))
            d[i][2] = m[2] * (up(here, 1) - down(here, 1))
        e = [d[a][b] if a == b else 0.5 * (d[a][b] + d[b][a]) for a, b in pairs]
        square = (e[0] * e[0] + e[1] * e[1] + e[2] * e[2]) + 2.0 * (e[3] * e[3] + e[4] * e[4] + e[5] * e[5])
        return e, jnp.sqrt(0.5 * square)

    def field_plane(x, _):
        m = [V[3 + c, x] for c in range(3)]
        e, mag = strains(lambda i, p: V[i, p], m, x)
        p = m[0][0:ny, 0:nz] * m[1][0:ny, 0:nz] * m[2][0:ny, 0:nz]
        dq = jnp.exp((-2.0 / 3.0) * jnp.log(p))
        Q[x] = dq
        D[jnp.clip(x - 2, 0, nx - 1)] = dq * mag[0:ny, 0:nz]
        for k, (a, b) in enumerate(pairs):
            put(k, x, V[a, x] * V[b, x])
            put(6 + k, x, mag * e[k])
        return 0

    def put(k, x, field):
        for t in range(zr // 128):
            tile = field[:, 128 * t : 128 * t + 128]
            F[k, x, t, 8 : 8 + yr] = tile
            F[k, x, t, 0:8] = tile[ny:yr]

    first = lane == 0
    last = lane == 127

    def smooth_plane(x, _):
        tiles_z = zr // 128
        for k in range(12):
            s = []
            for t in range(tiles_z):
                mid = F[k, x, t, 8 : 8 + ny]
                s.append((F[k, x, t, 7 : 7 + ny] + F[k, x, t, 9 : 9 + ny]) + (mid + mid))
            before = [pltpu.roll(a, 1, 1) for a in s]
            after = [pltpu.roll(a, 127, 1) for a in s]
            for t in range(nz // 128):
                lower = jnp.where(first, before[t - 1], before[t])
                upper = jnp.where(last, after[t + 1], after[t])
                G[k, x, :, 128 * t : 128 * t + 128] = (lower + upper) + (s[t] + s[t])
        return 0

    lax.fori_loop(2, nx + 2, velocity_plane, 0, unroll=8)
    lax.fori_loop(3, nx + 1, field_plane, 0, unroll=2)
    lax.fori_loop(3, nx + 1, smooth_plane, 0, unroll=2)
    land(lambda d: d[0] != 0)
    for f in range(6):
        fill_span(f, (0, 1, nx + 2, nx + 3))
    lax.fori_loop(0, 4, lambda i, c: velocity_plane(jnp.where(i < 2, i, nx + i), c), 0, unroll=4)
    lax.fori_loop(0, 4, lambda i, c: field_plane(jnp.where(i < 2, i + 1, nx + 4 - i), c), 0, unroll=2)
    lax.fori_loop(0, 4, lambda i, c: smooth_plane(jnp.where(i < 2, i + 1, nx + 4 - i), c), 0, unroll=2)

    save = pltpu.make_async_copy(D, d_out, sem_in.at[2])
    save.start()
    row = lax.broadcasted_iota(jnp.int32, (yr, zr), 0)
    has_lo = jnp.where(iy > 0, 1.0, 0.0)
    has_hi = jnp.where(iy < NY - 1, 1.0, 0.0)
    row_scale = jnp.where(row < ny, 1.0, jnp.where(row == ny, has_hi, has_lo)) * (1.0 / 64.0)

    def hat_plane(x, _):
        inside = jnp.where((x == 1) & (ix == 0), 0.0, jnp.where((x == nx + 2) & (ix == NX - 1), 0.0, 1.0))
        for c in range(3):
            mid = Gv[c, x]
            H[c, x] = (Gv[c, x - 1] + Gv[c, x + 1] + (mid + mid)) * (row_scale * inside)
        return 0

    lax.fori_loop(1, nx + 3, hat_plane, 0, unroll=2)

    lane_s = lax.broadcasted_iota(jnp.int32, (ny, 128), 1)

    def line_plane(x, sums):
        d = [[None] * 3 for _ in range(3)]
        hat = []
        for i in range(3):
            here = H[i, x]
            core = here[0:ny]
            hat.append(core[:, 0:nz])
            d[i][0] = V[3, x, 0:ny, 0:nz] * (H[i, x + 1, 0:ny, 0:nz] - H[i, x - 1, 0:ny, 0:nz])
            d[i][1] = V[4, x, 0:ny, 0:nz] * (up(here, 0) - down(here, 0))[0:ny, 0:nz]
            d[i][2] = V[5, x, 0:ny, 0:nz] * (up(core, 1) - down(core, 1))[:, 0:nz]
        e = [d[a][b] if a == b else 0.5 * (d[a][b] + d[b][a]) for a, b in pairs]
        square = (e[0] * e[0] + e[1] * e[1] + e[2] * e[2]) + 2.0 * (e[3] * e[3] + e[4] * e[4] + e[5] * e[5])
        mag2 = 2.0 * jnp.sqrt(0.5 * square)
        num = den = 0.0
        for k, (a, b) in enumerate(pairs):
            vv, ms = G[k, x], G[6 + k, x]
            vv = (G[k, x - 1] + G[k, x + 1] + (vv + vv)) * (1.0 / 64.0)
            ms = (G[6 + k, x - 1] + G[6 + k, x + 1] + (ms + ms)) * (1.0 / 128.0)
            leonard = vv - hat[a] * hat[b]
            model = ms - mag2 * e[k]
            n, m2 = leonard * model, model * model
            if pair_weight[k] != 1.0:
                n, m2 = pair_weight[k] * n, pair_weight[k] * m2
            num, den = num + n, den + m2
        dq2 = 2.0 * Q[x]
        num = num * dq2
        den = den * (dq2 * dq2)
        num = jnp.sum(num, axis=1, keepdims=True)
        den = jnp.sum(den, axis=1, keepdims=True)
        sums = jnp.where(lane_s == x - 2, num, sums)
        return jnp.where(lane_s == x + 62, den, sums)

    sums = lax.fori_loop(2, nx + 2, line_plane, jnp.zeros((ny, 128), jnp.float32), unroll=8)

    LS[iz] = sums
    def line_copy(o):
        return pltpu.make_async_remote_copy(
            src_ref=LS.at[iz], dst_ref=LS.at[iz], send_sem=lsend.at[o - 1], recv_sem=lrecv.at[o - 1],
            device_id=(ix, iy, lax.rem(iz + o, NZ)), device_id_type=MESH)
    def line_landing(o):
        src = lax.rem(iz - o + NZ, NZ)
        return pltpu.make_async_remote_copy(
            src_ref=LS.at[src], dst_ref=LS.at[src], send_sem=lsend.at[o - 1], recv_sem=lrecv.at[o - 1],
            device_id=(ix, iy, lax.rem(iz + o, NZ)), device_id_type=MESH)
    for o in range(1, NZ):
        line_copy(o).start()
    for o in range(1, NZ):
        line_landing(o).wait_recv()
    total = LS[0]
    for o in range(1, NZ):
        total = total + LS[o]
    cells = float(nz * NZ)
    line_num = total / cells
    line_den = pltpu.roll(total, 64, 1) / cells
    coef = line_num / (line_den + eps_line)
    masked = jnp.where(lane_s < nx, coef, -jnp.inf)
    here_max = masked[0:8]
    for r in range(8, ny, 8):
        here_max = jnp.maximum(here_max, masked[r : r + 8])
    me = ix * NY + iy
    PS[me] = here_max
    def peak_copy(j, a, b, landing):
        tx, ty = lax.rem(ix + a, NX), lax.rem(iy + b, NY)
        slot = me
        if landing:
            slot = lax.rem(ix - a + NX, NX) * NY + lax.rem(iy - b + NY, NY)
        return pltpu.make_async_remote_copy(
            src_ref=PS.at[slot], dst_ref=PS.at[slot], send_sem=psend.at[j], recv_sem=precv.at[j],
            device_id=(tx, ty, iz), device_id_type=MESH)
    for j, (a, b) in enumerate(plane_peers):
        peak_copy(j, a, b, False).start()
    for o in range(1, NZ):
        line_copy(o).wait_send()
    for j, (a, b) in enumerate(plane_peers):
        peak_copy(j, a, b, True).wait_recv()
    peak = PS[0]
    for j in range(1, NX * NY):
        peak = jnp.maximum(peak, PS[j])
    coef = jnp.minimum(coef, 0.5 * jnp.max(peak, axis=(0, 1), keepdims=True))
    coef_out[...] = coef
    save.wait()
    for j, (a, b) in enumerate(plane_peers):
        peak_copy(j, a, b, False).wait_send()
    for n, d in enumerate(offsets):
        def left(n=n, d=d):
            for c in copies(n, d):
                c.wait_send()
        when(exists(d), left)


def scale_kernel(D, coef, visc, coef_out):
    nx, ny = visc.shape[:2]
    lane = lax.broadcasted_iota(jnp.int32, (ny, 128), 1)
    table = coef[...]
    for x in range(nx):
        column = jnp.sum(jnp.where(lane == x, table, 0.0), axis=1, keepdims=True)
        visc[x] = D[x] * column
    coef_out[...] = table.T[0:nx, :]


def per_device(sizes, velocity, metric):
    nx, ny, nz = velocity.shape[1:]
    NX, NY, NZ = sizes
    yr, zr = ny + 8, nz + 128
    packed = -(-12 * nx // 128) * 128
    f32 = jnp.float32
    dmag, coef = pl.pallas_call(
        functools.partial(kernel, sizes),
        out_shape=(jax.ShapeDtypeStruct((nx, ny, nz), f32), jax.ShapeDtypeStruct((ny, 128), f32)),
        in_specs=[pl.BlockSpec(memory_space=pltpu.HBM)] * 2,
        out_specs=(pl.BlockSpec(memory_space=pltpu.HBM), pl.BlockSpec(memory_space=pltpu.VMEM)),
        scratch_shapes=[
            pltpu.VMEM((nx, ny, nz), f32),
            pltpu.VMEM((6, nx + 4, yr, zr), f32),
            pltpu.VMEM((3, nx + 4, yr, zr), f32),
            pltpu.VMEM((12, nx + 4, ny, nz), f32),
            pltpu.VMEM((3, nx + 4, yr, zr), f32),
            pltpu.VMEM((nx + 4, ny, nz), f32),
            pltpu.VMEM((12, nx + 4, zr // 128, 8 + yr, 128), f32),
            pltpu.VMEM((2, ny, packed), f32),
            pltpu.VMEM((2, 3, 3, ny, packed), f32),
            pltpu.VMEM((NZ, ny, 128), f32),
            pltpu.VMEM((NX * NY, 8, 128), f32),
            pltpu.SemaphoreType.DMA((3,)),
            pltpu.SemaphoreType.DMA((2 * len(offsets),)),
            pltpu.SemaphoreType.DMA((2 * len(offsets),)),
            pltpu.SemaphoreType.DMA((NZ,)),
            pltpu.SemaphoreType.DMA((NZ,)),
            pltpu.SemaphoreType.DMA((NX * NY,)),
            pltpu.SemaphoreType.DMA((NX * NY,)),
        ],
        compiler_params=pltpu.CompilerParams(collective_id=0, has_side_effects=True, vmem_limit_bytes=67043328 - 600 * 1024),
    )(velocity, metric)
    return pl.pallas_call(
        scale_kernel,
        out_shape=(jax.ShapeDtypeStruct((nx, ny, nz), f32), jax.ShapeDtypeStruct((nx, ny), f32)),
        in_specs=[pl.BlockSpec(memory_space=pltpu.VMEM)] * 2,
        out_specs=(pl.BlockSpec(memory_space=pltpu.VMEM),) * 2,
        compiler_params=pltpu.CompilerParams(vmem_limit_bytes=4 * 1024 * 1024),
    )(dmag, coef)


def solution(mesh):
    sizes = (mesh.shape["gx"], mesh.shape["gy"], mesh.shape["gz"])
    return jax.shard_map(
        functools.partial(per_device, sizes),
        mesh=mesh,
        in_specs=(P(None, "gx", "gy", "gz"), P(None, "gx", "gy", "gz")),
        out_specs=(P("gx", "gy", "gz"), P("gx", "gy")),
        check_vma=False,
    )
```

profile of v0, /device:TPU:0, one launch (start us, length us, event | category | flops | bytes accessed | tf_op | source)
XLA Modules:
  0.0 34.5 jit_solution(2184060195593724271)
XLA Ops:
  0.6 31.4 %shard_map.41 = (f32[16,16,256]{2,1,0:T(8,128)}, f32[16,128]{1,0:T(8,128)}) custom-call(f32[3,16,16,256]{3,2,1,0:T(8,128)} %vel.1, f32[3,16,16,256]{3,2,1,0:T(8,128)} %met.1), custom_call_target="tpu_custom_call" | custom-call | tf_op jit(solution)/shard_map/pallas_call | solution.py:381
  32.0 0.0 copy-start
  32.0 0.9 %copy-done = f32[16,16,256]{2,1,0:T(8,128)S(1)} copy-done((f32[16,16,256]{2,1,0:T(8,128)S(1)}, f32[16,16,256]{2,1,0:T(8,128)}, u32[]{:S(2)}) %copy-start) | copy-done | bytes 262168
  33.0 0.0 copy-start.1
  33.0 0.7 %copy-done.1 = f32[16,128]{1,0:T(8,128)S(1)} copy-done((f32[16,128]{1,0:T(8,128)S(1)}, f32[16,128]{1,0:T(8,128)}, u32[]{:S(2)}) %copy-start.1) | copy-done | bytes 8216
  33.7 0.8 %shard_map.42 = (f32[16,16,256]{2,1,0:T(8,128)}, f32[16,16]{1,0:T(8,128)}) custom-call(f32[16,16,256]{2,1,0:T(8,128)S(1)} %copy-done, f32[16,128]{1,0:T(8,128)S(1)} %copy-done.1), custom_call_target="tpu_custom_call" | custom-call | tf_op jit(solution)/shard_map/pallas_call | solution.py:408
Async XLA Ops:
  32.0 1.0 %copy-start = (f32[16,16,256]{2,1,0:T(8,128)S(1)}, f32[16,16,256]{2,1,0:T(8,128)}, u32[]{:S(2)}) copy-start(f32[16,16,256]{2,1,0:T(8,128)} %get-tuple-element.4.D) | copy-start | bytes 786436
  33.0 0.7 %copy-start.1 = (f32[16,128]{1,0:T(8,128)S(1)}, f32[16,128]{1,0:T(8,128)}, u32[]{:S(2)}) copy-start(f32[16,128]{1,0:T(8,128)} %get-tuple-element.5.coef) | copy-start | bytes 24580
where the time goes:
time: 34.7 us; the launch traced here: 34.5 us
  Pallas kernels  32.2 us (93%)
  local copies, waits for them, and re-layouts  1.64 us (5%)
  between operations  0.65 us (2%)
    pallas_call x1, Pallas kernels, per_device(): pl.pallas_call(functools.partial(kernel, sizes), out_shape=(jax.ShapeDtyp...  31.4 us
    unnamed x4, local copies, waits for them, and re-layouts  1.64 us
    pallas_call x1, Pallas kernels, per_device(): pl.pallas_call(scale_kernel, out_shape=(jax.ShapeDtypeStruct((nx, ny, nz)...  0.81 us

commit v1 on v0

v1 whole, which is shorter than its diff:
```python
import functools

import jax
import jax.numpy as jnp
from jax import lax
from jax.experimental import pallas as pl
from jax.experimental.pallas import tpu as pltpu
from jax.sharding import PartitionSpec as P

MESH = pl.DeviceIdType.MESH
pairs = ((0, 0), (1, 1), (2, 2), (0, 1), (0, 2), (1, 2))
eps_line = 1e-06
smallest = 1.1754944e-38
plane_offsets = [(dx, dy) for dx in (0, 1, -1) for dy in (0, 1, -1) if (dx, dy) != (0, 0)]
span_offsets = [(dx, dy, dz) for dz in (1, -1) for dx in (0, 1, -1) for dy in (0, 1, -1)]
G6 = 6


def root(s):
    return s * lax.rsqrt(jnp.maximum(s, smallest))


def tensor(d):
    f = [d[a][b] if a == b else d[a][b] + d[b][a] for a, b in pairs]
    square = (f[0] * f[0] + f[1] * f[1] + f[2] * f[2]) + 0.5 * (f[3] * f[3] + f[4] * f[4] + f[5] * f[5])
    return f, square


def model_sums(vv, ms, hat, dh, dq):
    f, square = tensor(dh)
    mh = root(8.0 * square)
    num = den = off = None
    for k, (a, b) in enumerate(pairs):
        leonard = vv[k] - hat[a] * hat[b]
        model = ms[k] - mh * f[k]
        n, m2 = leonard * model, model * model
        num = n if num is None else num + n
        if a == b:
            den = m2 if den is None else den + m2
        else:
            off = m2 if off is None else off + m2
    return num * dq, (den + 0.5 * off) * (dq * dq)


def kernel(sizes, vel, met, d_out, coef_out, V, Gv, G, H, Q, M, F, TE, E, EF, EG, PK, R, LS, PS, D, sem_in, send, recv, lsend, lrecv, psend, precv):
    NX, NY, NZ = sizes
    nx, ny, nz = vel.shape[1:]
    nt = nz // 128
    px = nx + 4
    starts = list(range(1, ny - 6, 8)) + [ny - 5]
    ix, iy, iz = lax.axis_index("gx"), lax.axis_index("gy"), lax.axis_index("gz")

    loads = []
    for k, src in enumerate((vel, met)):
        for t in range(nt):
            loads.append(pltpu.make_async_copy(
                src.at[:, :, :, 128 * t : 128 * t + 128],
                V.at[3 * k : 3 * k + 3, t, 2 : 2 + nx, 2 : 2 + ny, :],
                sem_in.at[k * nt + t]))
    for c in loads:
        c.start()

    def there(delta, i, n):
        return None if delta == 0 else (i + delta >= 0) & (i + delta < n)

    def exists(dx, dy):
        a, b = there(dx, ix, NX), there(dy, iy, NY)
        if a is None:
            return b
        return a if b is None else a & b

    def when(cond, fn):
        if cond is None:
            fn()
        else:
            pl.when(cond)(fn)

    def dev(d):
        return (ix + d[0], iy + d[1], lax.rem(iz + d[2] + NZ, NZ))

    barrier = pltpu.get_barrier_semaphore()
    expected = jnp.int32(0)
    for d in span_offsets + [(dx, dy, 0) for dx, dy in plane_offsets]:
        ok = exists(d[0], d[1])
        def sig(d=d):
            pl.semaphore_signal(barrier, inc=1, device_id=dev(d), device_id_type=MESH)
        when(ok, sig)
        expected = expected + (1 if ok is None else ok.astype(jnp.int32))
    for o in range(1, NZ):
        pl.semaphore_signal(barrier, inc=1, device_id=(ix, iy, lax.rem(iz + o, NZ)), device_id_type=MESH)
    plane_peers = [(a, b) for a in range(NX) for b in range(NY) if (a, b) != (0, 0)]
    for a, b in plane_peers:
        pl.semaphore_signal(barrier, inc=1, device_id=(lax.rem(ix + a, NX), lax.rem(iy + b, NY), iz), device_id_type=MESH)
    expected = expected + (NZ - 1 + len(plane_peers))

    z2 = jnp.zeros((2, 128), jnp.float32)
    for dx, p0 in ((-1, 0), (1, nx + 2)):
        def clear_planes(dx=dx, p0=p0):
            for f in range(6):
                for t in range(nt):
                    for p in (p0, p0 + 1):
                        V[f, t, p] = jnp.zeros((ny + 8, 128), jnp.float32)
            for s in range(2):
                for k in range(2):
                    R[s, dx + 1, k] = jnp.zeros((ny + 8, 128), jnp.float32)
        pl.when(jnp.logical_not(there(dx, ix, NX)))(clear_planes)
    for dy, r0 in ((-1, 0), (1, ny + 2)):
        def clear_rows(r0=r0):
            def body(p, _):
                for f in range(6):
                    for t in range(nt):
                        V[f, t, p, r0 : r0 + 2, :] = z2
                return 0
            lax.fori_loop(0, px, body, 0)
            for s in range(2):
                for f in range(6):
                    TE[s, f, r0 : r0 + 2, :] = z2
                for dxi in range(3):
                    for k in range(2):
                        R[s, dxi, k, r0 : r0 + 2, :] = z2
        pl.when(jnp.logical_not(there(dy, iy, NY)))(clear_rows)

    for c in loads:
        c.wait()

    lane = lax.broadcasted_iota(jnp.int32, (ny, 128), 1)
    group = (lane * 43) >> 8
    inner = lane - G6 * group
    lane8, group8, inner8 = lane[0:8], group[0:8], inner[0:8]

    def lroll(a, s):
        s = s % 128
        return pltpu.roll(a, s, 1) if s else a

    for f in range(6):
        for s in range(2):
            acc = jnp.zeros((ny, 128), jnp.float32)
            for p in range(2, 2 + nx):
                tile = V[f, 0 if s == 0 else nt - 1, p, 2 : 2 + ny, :]
                acc = jnp.where(group == p, lroll(tile, G6 * p - (0 if s == 0 else 122)), acc)
            TE[s, f, 2 : 2 + ny, :] = acc
    for s in range(2):
        for k in range(2):
            parts = [lroll(TE[s, 3 * k + c, 2 : 2 + ny, :], 2 * c - (0 if s == 0 else 4)) for c in range(3)]
            PK[s, k] = jnp.where(inner < 2, parts[0], jnp.where(inner < 4, parts[1], parts[2]))

    pl.semaphore_wait(barrier, expected)

    def span_x(dx, deep):
        if dx == 0:
            return (2, 2, nx)
        if dx == 1:
            return (nx, 0, 2) if deep else (nx + 1, 1, 1)
        return (2, nx + 2, 2) if deep else (2, nx + 2, 1)

    def span_y(dy, deep):
        if dy == 0:
            return (2, 2, ny)
        if dy == 1:
            return (ny, 0, 2) if deep else (ny + 1, 1, 1)
        return (2, ny + 2, 2) if deep else (2, ny + 2, 1)

    def remote(src, dst, j, d):
        return pltpu.make_async_remote_copy(src_ref=src, dst_ref=dst, send_sem=send.at[j], recv_sem=recv.at[j], device_id=dev(d), device_id_type=MESH)

    def span_copy(n):
        dx, dy, dz = d = span_offsets[n]
        s = 1 if dz == 1 else 0
        ys, yd, yn = span_y(dy, True)
        return remote(PK.at[s, :, ys - 2 : ys - 2 + yn, :], R.at[s, 1 - dx, :, yd : yd + yn, :], n, d)

    def plane_copies(n):
        dx, dy = plane_offsets[n]
        d = (dx, dy, 0)
        base = len(span_offsets) + 3 * n
        out = []
        for k in range(2):
            xs, xd, xn = span_x(dx, k == 0)
            ys, yd, yn = span_y(dy, k == 0)
            f0 = 3 * k
            out.append(remote(V.at[f0 : f0 + 3, :, xs : xs + xn, ys : ys + yn, :], V.at[f0 : f0 + 3, :, xd : xd + xn, yd : yd + yn, :], base + k, d))
        if dx == 0:
            ys, yd, yn = span_y(dy, True)
            out.append(remote(TE.at[:, :, ys : ys + yn, :], TE.at[:, :, yd : yd + yn, :], base + 2, d))
        return out

    everything = [(d, (lambda n=n: [span_copy(n)])) for n, d in enumerate(span_offsets)]
    everything += [((dx, dy, 0), (lambda n=n: plane_copies(n))) for n, (dx, dy) in enumerate(plane_offsets)]
    for d, make in everything:
        def go(make=make):
            for c in make():
                c.start()
        when(exists(d[0], d[1]), go)

    def land(wanted):
        for d, make in everything:
            if wanted(d):
                def arrive(make=make):
                    for c in make():
                        c.wait_recv()
                when(exists(-d[0], -d[1]), arrive)

    first, last = lane8 == 0, lane8 == 127

    def zup(a):
        r = [pltpu.roll(v, 127, 1) for v in a]
        return [jnp.where(last, r[(t + 1) % nt], r[t]) for t in range(nt)]

    def zdown(a):
        r = [pltpu.roll(v, 1, 1) for v in a]
        return [jnp.where(first, r[t - 1], r[t]) for t in range(nt)]

    def zsmooth(a):
        t1 = [v + w for v, w in zip(a, zup(a))]
        return [v + w for v, w in zip(t1, zdown(t1))]

    def field_plane(x, _):
        for r in starts:
            here = slice(r, r + 8)
            m = [[V[3 + c, t, x, here, :] for c in range(3)] for t in range(nt)]
            u, d = [], [[[None] * 3 for _ in range(3)] for _ in range(nt)]
            for i in range(3):
                mid = [V[i, t, x, here, :] for t in range(nt)]
                u.append(mid)
                hi, lo = zup(mid), zdown(mid)
                for t in range(nt):
                    above, below = V[i, t, x, r + 1 : r + 9, :], V[i, t, x, r - 1 : r + 7, :]
                    Gv[i, t, x, here, :] = (mid[t] + mid[t]) + (above + below)
                    d[t][i][0] = m[t][0] * (V[i, t, x + 1, here, :] - V[i, t, x - 1, here, :])
                    d[t][i][1] = m[t][1] * (above - below)
                    d[t][i][2] = m[t][2] * (hi[t] - lo[t])
            for t in range(nt):
                f, square = tensor(d[t])
                mag = root(0.5 * square)
                dq = jnp.exp2((-2.0 / 3.0) * jnp.log2(m[t][0] * m[t][1] * m[t][2]))
                Q[t, x, here, :] = dq
                M[t, x, here, :] = dq * mag
                for k, (a, b) in enumerate(pairs):
                    F[k, t, x, here, :] = u[a][t] * u[b][t]
                    F[6 + k, t, x, here, :] = mag * f[k]
        return 0

    def velocity_plane(x, _):
        for c in range(3):
            for t in range(nt):
                for r in starts:
                    mid = V[c, t, x, r : r + 8, :]
                    Gv[c, t, x, r : r + 8, :] = (mid + mid) + (V[c, t, x, r - 1 : r + 7, :] + V[c, t, x, r + 1 : r + 9, :])
        return 0

    def smooth_plane(x, _):
        for k in range(12):
            for t in range(nt):
                for r in range(0, ny, 8):
                    mid = F[k, t, x, r + 2 : r + 10, :]
                    G[k, t, x, r : r + 8, :] = (mid + mid) + (F[k, t, x, r + 1 : r + 9, :] + F[k, t, x, r + 3 : r + 11, :])
        return 0

    has_lo = jnp.where(iy > 0, 0.125, 0.0)
    has_hi = jnp.where(iy < NY - 1, 0.125, 0.0)
    rows8 = lax.broadcasted_iota(jnp.int32, (8, 128), 0)

    def row_scale(r):
        idx = rows8 + r
        return jnp.where(idx < 2, has_lo, jnp.where(idx < ny + 2, 0.125, has_hi))

    def hat_plane(x, _):
        inside = jnp.where((x == 1) & (ix == 0), 0.0, jnp.where((x == nx + 2) & (ix == NX - 1), 0.0, 1.0))
        for r in starts:
            scale = row_scale(r) * inside
            for c in range(3):
                s = []
                for t in range(nt):
                    mid = Gv[c, t, x, r : r + 8, :]
                    s.append((mid + mid) + (Gv[c, t, x - 1, r : r + 8, :] + Gv[c, t, x + 1, r : r + 8, :]))
                s = zsmooth(s)
                for t in range(nt):
                    H[c, t, x, r : r + 8, :] = s[t] * scale
        return 0

    keep = [None] * nt
    keep[0] = lane8 >= 2
    keep[nt - 1] = (lane8 < 126) if nt > 1 else (lane8 >= 2) & (lane8 < 126)

    def line_plane(x, sums):
        out = []
        for b, r in enumerate(range(0, ny, 8)):
            here = slice(r + 2, r + 10)
            filtered = []
            for k in range(12):
                s = []
                for t in range(nt):
                    mid = G[k, t, x, r : r + 8, :]
                    s.append((mid + mid) + (G[k, t, x - 1, r : r + 8, :] + G[k, t, x + 1, r : r + 8, :]))
                filtered.append(zsmooth(s))
            hat, d = [], [[[None] * 3 for _ in range(3)] for _ in range(nt)]
            m = [[V[3 + c, t, x, here, :] for c in range(3)] for t in range(nt)]
            for i in range(3):
                mid = [H[i, t, x, here, :] for t in range(nt)]
                hat.append(mid)
                hi, lo = zup(mid), zdown(mid)
                for t in range(nt):
                    d[t][i][0] = m[t][0] * (H[i, t, x + 1, here, :] - H[i, t, x - 1, here, :])
                    d[t][i][1] = m[t][1] * (H[i, t, x, r + 3 : r + 11, :] - H[i, t, x, r + 1 : r + 9, :])
                    d[t][i][2] = m[t][2] * (hi[t] - lo[t])
            num = den = 0.0
            for t in range(nt):
                n, e = model_sums([filtered[k][t] for k in range(6)], [filtered[6 + k][t] for k in range(6)], [h[t] for h in hat], d[t], Q[t, x, here, :])
                if keep[t] is not None:
                    n, e = jnp.where(keep[t], n, 0.0), jnp.where(keep[t], e, 0.0)
                num, den = num + n, den + e
            num = jnp.sum(num, axis=1, keepdims=True)
            den = jnp.sum(den, axis=1, keepdims=True)
            acc = jnp.where(lane8 == G6 * x + 2, num, sums[b])
            out.append(jnp.where(lane8 == G6 * x + 4, den, acc))
        return tuple(out)

    land(lambda d: d[0] == 0 and d[2] == 0)
    lax.fori_loop(3, nx + 1, field_plane, 0, unroll=2)
    lax.fori_loop(0, 2, lambda i, c: velocity_plane(2 + i * (nx - 1), c), 0)
    lax.fori_loop(3, nx + 1, smooth_plane, 0, unroll=2)
    lax.fori_loop(3, nx + 1, hat_plane, 0, unroll=2)
    sums = tuple(jnp.zeros((8, 128), jnp.float32) for _ in range(0, ny, 8))
    sums = lax.fori_loop(4, nx, line_plane, sums)
    land(lambda d: d[0] != 0 and d[2] == 0)

    def edges(per_side):
        return lambda i: jnp.where(i < len(per_side), per_side[0] + i, nx + 3 - per_side[-1] + i - len(per_side))
    near, inner_planes = edges([1, 2]), edges([2, 3])
    lax.fori_loop(0, 4, lambda i, c: field_plane(near(i), c), 0)
    lax.fori_loop(0, 2, lambda i, c: velocity_plane(i * (nx + 3), c), 0)
    lax.fori_loop(0, 4, lambda i, c: smooth_plane(near(i), c), 0)
    lax.fori_loop(0, 4, lambda i, c: hat_plane(near(i), c), 0)
    sums = lax.fori_loop(0, 4, lambda i, c: line_plane(inner_planes(i), c), sums)
    land(lambda d: d[2] != 0)

    yr = ny + 8
    lane_r = lax.broadcasted_iota(jnp.int32, (yr, 128), 1)
    group_r = (lane_r * 43) >> 8
    inner_r = lane_r - G6 * group_r
    rows_r = lax.broadcasted_iota(jnp.int32, (yr, 128), 0)
    outside = ((group_r == 1) & (ix == 0)) | ((group_r == nx + 2) & (ix == NX - 1))
    outside = outside | ((rows_r < 2) & (iy == 0)) | ((rows_r >= ny + 2) & (iy == NY - 1))
    scale_r = jnp.where(outside, 0.0, 0.125)
    enum, eden = 0.0, 0.0
    fixes = []
    for s in range(2):
        mixed = []
        for k in range(2):
            far = jnp.where(lane_r < 2 * G6, lroll(R[1 - s, 0, k], -G6 * nx), R[1 - s, 1, k])
            mixed.append(jnp.where(lane_r >= G6 * (nx + 2), lroll(R[1 - s, 2, k], G6 * nx), far))
        fields = []
        for f in range(6):
            own = TE[s, f]
            for p in (0, 1, nx + 2, nx + 3):
                if f >= 3 and p in (0, nx + 3):
                    continue
                tile = V[f, 0 if s == 0 else nt - 1, p]
                own = jnp.where(group_r == p, lroll(tile, G6 * p - (0 if s == 0 else 122)), own)
            c = f % 3
            if s == 0:
                fields.append(jnp.where(inner_r < 2, lroll(mixed[f // 3], -2 * c), lroll(own, 2)))
            else:
                fields.append(jnp.where(inner_r >= 4, lroll(mixed[f // 3], 4 - 2 * c), lroll(own, -2)))
        u, m = fields[0:3], fields[3:6]
        for f in range(6):
            E[s, f] = fields[f]
        def shift(a, n):
            return lroll(a, -n)
        d = [[None] * 3 for _ in range(3)]
        for i in range(3):
            d[i][0] = m[0] * (shift(u[i], G6) - shift(u[i], -G6))
            d[i][1] = m[1] * (pltpu.roll(u[i], yr - 1, 0) - pltpu.roll(u[i], 1, 0))
            d[i][2] = m[2] * (shift(u[i], 1) - shift(u[i], -1))
        f, square = tensor(d)
        mag = root(0.5 * square)
        dq = jnp.exp2((-2.0 / 3.0) * jnp.log2(m[0] * m[1] * m[2]))
        EF[s, 15] = dq
        EF[s, 16] = dq * mag
        for c in range(3):
            EF[s, 12 + c] = u[c]
        for k, (a, b) in enumerate(pairs):
            EF[s, k] = u[a] * u[b]
            EF[s, 6 + k] = mag * f[k]
        def lanes_smooth(a):
            b = (a + a) + (shift(a, G6) + shift(a, -G6))
            return (b + b) + (shift(b, 1) + shift(b, -1))
        for c in range(3):
            y = (u[c] + u[c]) + (pltpu.roll(u[c], yr - 1, 0) + pltpu.roll(u[c], 1, 0))
            EG[s, c] = lanes_smooth(y) * scale_r
        own = slice(2, 2 + ny)
        filtered = []
        for k in range(12):
            mid = EF[s, k, own, :]
            filtered.append(lanes_smooth((mid + mid) + (EF[s, k, 1 : 1 + ny, :] + EF[s, k, 3 : 3 + ny, :])))
        hat, dh = [], [[None] * 3 for _ in range(3)]
        me = [E[s, 3 + c, own, :] for c in range(3)]
        for i in range(3):
            mid = EG[s, i, own, :]
            hat.append(mid)
            dh[i][0] = me[0] * (shift(mid, G6) - shift(mid, -G6))
            dh[i][1] = me[1] * (EG[s, i, 3 : 3 + ny, :] - EG[s, i, 1 : 1 + ny, :])
            dh[i][2] = me[2] * (shift(mid, 1) - shift(mid, -1))
        n, e = model_sums(filtered[0:6], filtered[6:12], hat, dh, EF[s, 15, own, :])
        enum, eden = enum + n, eden + e
    enum = enum + lroll(enum, -1)
    eden = lroll(eden + lroll(eden, -1), 2)
    used = (group >= 2) & (group < nx + 2)
    extra = jnp.where(used & (inner == 2), enum, jnp.where(used & (inner == 4), eden, 0.0))
    LS[iz] = jnp.concatenate(sums, axis=0) + extra

    def line_copy(o):
        return pltpu.make_async_remote_copy(
            src_ref=LS.at[iz], dst_ref=LS.at[iz], send_sem=lsend.at[o - 1], recv_sem=lrecv.at[o - 1],
            device_id=(ix, iy, lax.rem(iz + o, NZ)), device_id_type=MESH)
    def line_landing(o):
        src = lax.rem(iz - o + NZ, NZ)
        return pltpu.make_async_remote_copy(
            src_ref=LS.at[src], dst_ref=LS.at[src], send_sem=lsend.at[o - 1], recv_sem=lrecv.at[o - 1],
            device_id=(ix, iy, lax.rem(iz + o, NZ)), device_id_type=MESH)
    for o in range(1, NZ):
        line_copy(o).start()

    lo_fix, hi_fix = EF[0, 16, 2 : 2 + ny, :], EF[1, 16, 2 : 2 + ny, :]
    for x in range(nx):
        p = x + 2
        for t in range(nt):
            tile = M[t, p, 2 : 2 + ny, :]
            if t == 0:
                tile = jnp.where(lane == 0, lroll(lo_fix, -(G6 * p + 2)), tile)
            if t == nt - 1:
                tile = jnp.where(lane == 127, lroll(hi_fix, 127 - (G6 * p + 3)), tile)
            D[x, :, 128 * t : 128 * t + 128] = tile
    save = pltpu.make_async_copy(D, d_out, sem_in.at[2 * nt])
    save.start()

    for o in range(1, NZ):
        line_landing(o).wait_recv()
    total = LS[0]
    for o in range(1, NZ):
        total = total + LS[o]
    unit = 4096.0 * nz * NZ
    coef = (total / unit) / (lroll(total, -2) / unit + eps_line)
    masked = jnp.where(used & (inner == 2), coef, -jnp.inf)
    here_max = masked[0:8]
    for r in range(8, ny, 8):
        here_max = jnp.maximum(here_max, masked[r : r + 8])
    me = ix * NY + iy
    PS[me] = here_max
    def peak_copy(j, a, b, landing):
        tx, ty = lax.rem(ix + a, NX), lax.rem(iy + b, NY)
        slot = me
        if landing:
            slot = lax.rem(ix - a + NX, NX) * NY + lax.rem(iy - b + NY, NY)
        return pltpu.make_async_remote_copy(
            src_ref=PS.at[slot], dst_ref=PS.at[slot], send_sem=psend.at[j], recv_sem=precv.at[j],
            device_id=(tx, ty, iz), device_id_type=MESH)
    for j, (a, b) in enumerate(plane_peers):
        peak_copy(j, a, b, False).start()
    for o in range(1, NZ):
        line_copy(o).wait_send()
    for d, make in everything:
        def left(make=make):
            for c in make():
                c.wait_send()
        when(exists(d[0], d[1]), left)
    for j, (a, b) in enumerate(plane_peers):
        peak_copy(j, a, b, True).wait_recv()
    peak = PS[0]
    for j in range(1, NX * NY):
        peak = jnp.maximum(peak, PS[j])
    coef_out[...] = jnp.minimum(coef, 0.5 * jnp.max(peak, axis=(0, 1), keepdims=True))
    save.wait()
    for j, (a, b) in enumerate(plane_peers):
        peak_copy(j, a, b, False).wait_send()


def scale_kernel(D, coef, visc, coef_out):
    nx, ny = visc.shape[:2]
    lane = lax.broadcasted_iota(jnp.int32, (ny, 128), 1)
    table = coef[...]
    turned = table.T
    for x in range(nx):
        at = G6 * (x + 2) + 2
        column = jnp.sum(jnp.where(lane == at, table, 0.0), axis=1, keepdims=True)
        visc[x] = D[x] * column
        coef_out[x : x + 1, :] = turned[at : at + 1, :]


def per_device(sizes, velocity, metric):
    nx, ny, nz = velocity.shape[1:]
    NX, NY, NZ = sizes
    assert nz % 128 == 0 and ny % 8 == 0 and G6 * (nx + 4) <= 128 and nx >= 6
    nt, px, yr = nz // 128, nx + 4, ny + 8
    f32 = jnp.float32
    copies = len(span_offsets) + 3 * len(plane_offsets)
    dmag, coef = pl.pallas_call(
        functools.partial(kernel, sizes),
        out_shape=(jax.ShapeDtypeStruct((nx, ny, nz), f32), jax.ShapeDtypeStruct((ny, 128), f32)),
        in_specs=[pl.BlockSpec(memory_space=pltpu.HBM)] * 2,
        out_specs=(pl.BlockSpec(memory_space=pltpu.HBM), pl.BlockSpec(memory_space=pltpu.VMEM)),
        scratch_shapes=[
            pltpu.VMEM((6, nt, px, yr, 128), f32),
            pltpu.VMEM((3, nt, px, yr, 128), f32),
            pltpu.VMEM((12, nt, px, ny, 128), f32),
            pltpu.VMEM((3, nt, px, yr, 128), f32),
            pltpu.VMEM((nt, px, yr, 128), f32),
            pltpu.VMEM((nt, px, yr, 128), f32),
            pltpu.VMEM((12, nt, px, yr, 128), f32),
            pltpu.VMEM((2, 6, yr, 128), f32),
            pltpu.VMEM((2, 6, yr, 128), f32),
            pltpu.VMEM((2, 17, yr, 128), f32),
            pltpu.VMEM((2, 3, yr, 128), f32),
            pltpu.VMEM((2, 2, ny, 128), f32),
            pltpu.VMEM((2, 3, 2, yr, 128), f32),
            pltpu.VMEM((NZ, ny, 128), f32),
            pltpu.VMEM((NX * NY, 8, 128), f32),
            pltpu.VMEM((nx, ny, nz), f32),
            pltpu.SemaphoreType.DMA((2 * nt + 1,)),
            pltpu.SemaphoreType.DMA((copies,)),
            pltpu.SemaphoreType.DMA((copies,)),
            pltpu.SemaphoreType.DMA((NZ,)),
            pltpu.SemaphoreType.DMA((NZ,)),
            pltpu.SemaphoreType.DMA((NX * NY,)),
            pltpu.SemaphoreType.DMA((NX * NY,)),
        ],
        compiler_params=pltpu.CompilerParams(collective_id=0, has_side_effects=True, vmem_limit_bytes=67043328 - 600 * 1024),
    )(velocity, metric)
    return pl.pallas_call(
        scale_kernel,
        out_shape=(jax.ShapeDtypeStruct((nx, ny, nz), f32), jax.ShapeDtypeStruct((nx, ny), f32)),
        in_specs=[pl.BlockSpec(memory_space=pltpu.VMEM)] * 2,
        out_specs=(pl.BlockSpec(memory_space=pltpu.VMEM),) * 2,
        compiler_params=pltpu.CompilerParams(vmem_limit_bytes=4 * 1024 * 1024),
    )(dmag, coef)


def solution(mesh):
    sizes = (mesh.shape["gx"], mesh.shape["gy"], mesh.shape["gz"])
    return jax.shard_map(
        functools.partial(per_device, sizes),
        mesh=mesh,
        in_specs=(P(None, "gx", "gy", "gz"), P(None, "gx", "gy", "gz")),
        out_specs=(P("gx", "gy", "gz"), P("gx", "gy")),
        check_vma=False,
    )
```

time: 34.7 us -> 32 us (0.922)
  Pallas kernels: 32.2 us -> 29.5 us
    pallas_call x1, Pallas kernels: 31.4 us -> 28.7 us  [per_device(): pl.pallas_call(functools.partial(kernel, sizes), out_shape=(jax.ShapeDtyp...]
where the time goes in v1:
time: 32 us; the launch traced here: 31.8 us
  Pallas kernels  29.5 us (92%)
  local copies, waits for them, and re-layouts  1.64 us (5%)
  between operations  0.65 us (2%)
    pallas_call x1, Pallas kernels, per_device(): pl.pallas_call(functools.partial(kernel, sizes), out_shape=(jax.ShapeDtyp...  28.7 us
    unnamed x4, local copies, waits for them, and re-layouts  1.64 us
    pallas_call x1, Pallas kernels, per_device(): pl.pallas_call(scale_kernel, out_shape=(jax.ShapeDtypeStruct((nx, ny, nz)...  0.84 us

profile of v1, /device:TPU:0, one launch (start us, length us, event | category | flops | bytes accessed | tf_op | source)
XLA Modules:
  0.0 31.8 jit_solution(5088845954014670964)
XLA Ops:
  0.6 28.7 %shard_map.41 = (f32[16,16,256]{2,1,0:T(8,128)}, f32[16,128]{1,0:T(8,128)}) custom-call(f32[3,16,16,256]{3,2,1,0:T(8,128)} %vel.1, f32[3,16,16,256]{3,2,1,0:T(8,128)} %met.1), custom_call_target="tpu_custom_call" | custom-call | tf_op jit(solution)/shard_map/pallas_call | solution.py:497
  29.3 0.0 copy-start
  29.3 0.9 %copy-done = f32[16,16,256]{2,1,0:T(8,128)S(1)} copy-done((f32[16,16,256]{2,1,0:T(8,128)S(1)}, f32[16,16,256]{2,1,0:T(8,128)}, u32[]{:S(2)}) %copy-start) | copy-done | bytes 262168
  30.3 0.0 copy-start.1
  30.3 0.7 %copy-done.1 = f32[16,128]{1,0:T(8,128)S(1)} copy-done((f32[16,128]{1,0:T(8,128)S(1)}, f32[16,128]{1,0:T(8,128)}, u32[]{:S(2)}) %copy-start.1) | copy-done | bytes 8216
  31.0 0.8 %shard_map.42 = (f32[16,16,256]{2,1,0:T(8,128)}, f32[16,16]{1,0:T(8,128)}) custom-call(f32[16,16,256]{2,1,0:T(8,128)S(1)} %copy-done, f32[16,128]{1,0:T(8,128)S(1)} %copy-done.1), custom_call_target="tpu_custom_call" | custom-call | tf_op jit(solution)/shard_map/pallas_call | solution.py:529
Async XLA Ops:
  29.3 1.0 %copy-start = (f32[16,16,256]{2,1,0:T(8,128)S(1)}, f32[16,16,256]{2,1,0:T(8,128)}, u32[]{:S(2)}) copy-start(f32[16,16,256]{2,1,0:T(8,128)} %get-tuple-element.4.D) | copy-start | bytes 786436
  30.3 0.7 %copy-start.1 = (f32[16,128]{1,0:T(8,128)S(1)}, f32[16,128]{1,0:T(8,128)}, u32[]{:S(2)}) copy-start(f32[16,128]{1,0:T(8,128)} %get-tuple-element.5.coef) | copy-start | bytes 24580

commit v2 on v1

--- a/solution.py
+++ b/solution.py
@@ -13,6 +13,7 @@
 smallest = 1.1754944e-38
 plane_offsets = [(dx, dy) for dx in (0, 1, -1) for dy in (0, 1, -1) if (dx, dy) != (0, 0)]
 span_offsets = [(dx, dy, dz) for dz in (1, -1) for dx in (0, 1, -1) for dy in (0, 1, -1)]
+chunks = 4
 G6 = 6
 
 
@@ -42,7 +43,7 @@
     return num * dq, (den + 0.5 * off) * (dq * dq)
 
 
-def kernel(sizes, vel, met, d_out, coef_out, V, Gv, G, H, Q, M, F, TE, E, EF, EG, PK, R, LS, PS, D, sem_in, send, recv, lsend, lrecv, psend, precv):
+def kernel(sizes, vel, met, d_out, coef_out, V, Gv, G, H, Q, M, F, TE, E, EF, EG, PK, R, LS, PS, D, W, sem_in, send, recv, lsend, lrecv, psend, precv):
     NX, NY, NZ = sizes
     nx, ny, nz = vel.shape[1:]
     nt = nz // 128
@@ -169,19 +170,26 @@
         ys, yd, yn = span_y(dy, True)
         return remote(PK.at[s, :, ys - 2 : ys - 2 + yn, :], R.at[s, 1 - dx, :, yd : yd + yn, :], n, d)
 
-    def plane_copies(n):
+    chunk = nx // chunks
+
+    def plane_copies(n, part=None):
         dx, dy = plane_offsets[n]
         d = (dx, dy, 0)
-        base = len(span_offsets) + 3 * n
+        base = len(span_offsets) + (2 * chunks + 1) * n
         out = []
-        for k in range(2):
-            xs, xd, xn = span_x(dx, k == 0)
-            ys, yd, yn = span_y(dy, k == 0)
-            f0 = 3 * k
-            out.append(remote(V.at[f0 : f0 + 3, :, xs : xs + xn, ys : ys + yn, :], V.at[f0 : f0 + 3, :, xd : xd + xn, yd : yd + yn, :], base + k, d))
-        if dx == 0:
+        for c in range(chunks if dx == 0 else 1):
+            if part is not None and c != part:
+                continue
+            for k in range(2):
+                xs, xd, xn = span_x(dx, k == 0)
+                if dx == 0:
+                    xs, xd, xn = 2 + c * chunk, 2 + c * chunk, chunk
+                ys, yd, yn = span_y(dy, k == 0)
+                f0 = 3 * k
+                out.append(remote(V.at[f0 : f0 + 3, :, xs : xs + xn, ys : ys + yn, :], V.at[f0 : f0 + 3, :, xd : xd + xn, yd : yd + yn, :], base + 2 * c + k, d))
+        if dx == 0 and part in (None, chunks - 1):
             ys, yd, yn = span_y(dy, True)
-            out.append(remote(TE.at[:, :, ys : ys + yn, :], TE.at[:, :, yd : yd + yn, :], base + 2, d))
+            out.append(remote(TE.at[:, :, ys : ys + yn, :], TE.at[:, :, yd : yd + yn, :], base + 2 * chunks, d))
         return out
 
     everything = [(d, (lambda n=n: [span_copy(n)])) for n, d in enumerate(span_offsets)]
@@ -211,8 +219,7 @@
         return [jnp.where(first, r[t - 1], r[t]) for t in range(nt)]
 
     def zsmooth(a):
-        t1 = [v + w for v, w in zip(a, zup(a))]
-        return [v + w for v, w in zip(t1, zdown(t1))]
+        return [(v + v) + (w + q) for v, w, q in zip(a, zup(a), zdown(a))]
 
     def field_plane(x, _):
         for r in starts:
@@ -248,12 +255,34 @@
                     Gv[c, t, x, r : r + 8, :] = (mid + mid) + (V[c, t, x, r - 1 : r + 7, :] + V[c, t, x, r + 1 : r + 9, :])
         return 0
 
+    zi = lax.broadcasted_iota(jnp.int32, (nz, nz), 0)
+    zj = lax.broadcasted_iota(jnp.int32, (nz, nz), 1)
+    gap = jnp.abs(zi - zj)
+    W[...] = jnp.where(gap == 0, 2.0, jnp.where((gap == 1) | (gap == nz - 1), 1.0, 0.0)).astype(jnp.bfloat16)
+
+    def banded(a):
+        w = W[...]
+        hi = a.astype(jnp.bfloat16)
+        rest = a - hi.astype(jnp.float32)
+        mid = rest.astype(jnp.bfloat16)
+        low = (rest - mid.astype(jnp.float32)).astype(jnp.bfloat16)
+        n = a.shape[0]
+        out = jnp.dot(jnp.concatenate([hi, mid, low], axis=0), w, preferred_element_type=jnp.float32)
+        return out[0:n] + (out[n : 2 * n] + out[2 * n :])
+
     def smooth_plane(x, _):
-        for k in range(12):
-            for t in range(nt):
-                for r in range(0, ny, 8):
-                    mid = F[k, t, x, r + 2 : r + 10, :]
-                    G[k, t, x, r : r + 8, :] = (mid + mid) + (F[k, t, x, r + 1 : r + 9, :] + F[k, t, x, r + 3 : r + 11, :])
+        for k0 in (0,):
+            s = []
+            for k in range(12):
+                row = []
+                for t in range(nt):
+                    mid = F[k, t, x, 2 : 2 + ny, :]
+                    row.append((mid + mid) + (F[k, t, x, 1 : 1 + ny, :] + F[k, t, x, 3 : 3 + ny, :]))
+                s.append(jnp.concatenate(row, axis=1))
+            s = banded(jnp.concatenate(s, axis=0))
+            for k in range(12):
+                for t in range(nt):
+                    G[k, t, x] = s[(k - k0) * ny : (k - k0 + 1) * ny, 128 * t : 128 * t + 128]
         return 0
 
     has_lo = jnp.where(iy > 0, 0.125, 0.0)
@@ -292,7 +321,7 @@
                 for t in range(nt):
                     mid = G[k, t, x, r : r + 8, :]
                     s.append((mid + mid) + (G[k, t, x - 1, r : r + 8, :] + G[k, t, x + 1, r : r + 8, :]))
-                filtered.append(zsmooth(s))
+                filtered.append(s)
             hat, d = [], [[[None] * 3 for _ in range(3)] for _ in range(nt)]
             m = [[V[3 + c, t, x, here, :] for c in range(3)] for t in range(nt)]
             for i in range(3):
@@ -315,23 +344,55 @@
             out.append(jnp.where(lane8 == G6 * x + 4, den, acc))
         return tuple(out)
 
-    land(lambda d: d[0] == 0 and d[2] == 0)
-    lax.fori_loop(3, nx + 1, field_plane, 0, unroll=2)
-    lax.fori_loop(0, 2, lambda i, c: velocity_plane(2 + i * (nx - 1), c), 0)
-    lax.fori_loop(3, nx + 1, smooth_plane, 0, unroll=2)
-    lax.fori_loop(3, nx + 1, hat_plane, 0, unroll=2)
+    def land_chunk(c):
+        for n, (dx, dy) in enumerate(plane_offsets):
+            if dx == 0:
+                def arrive(n=n):
+                    for cp in plane_copies(n, c):
+                        cp.wait_recv()
+                when(exists(0, -dy), arrive)
+
+    def step(i, sums, smooth=True, hat=True, line=True):
+        if line:
+            sums = line_plane(i - 4, sums)
+        if hat:
+            hat_plane(i - 2, 0)
+        if smooth:
+            smooth_plane(i - 1, 0)
+        field_plane(i, 0)
+        return sums
+
     sums = tuple(jnp.zeros((8, 128), jnp.float32) for _ in range(0, ny, 8))
-    sums = lax.fori_loop(4, nx, line_plane, sums)
+    for c in range(chunks):
+        land_chunk(c)
+        lo = 3 if c == 0 else chunk * c + 1
+        hi = chunk * (c + 1)
+        if c == 0:
+            velocity_plane(2, 0)
+            step(3, sums, False, False, False)
+            lax.fori_loop(4, hi + 1, lambda i, q: step(i, q, True, False, False), ())
+        elif c == 1:
+            lax.fori_loop(lo, min(hi + 1, 8), lambda i, q: step(i, q, True, True, False), ())
+            sums = lax.fori_loop(8, hi + 1, step, sums)
+        else:
+            sums = lax.fori_loop(lo, hi + 1, step, sums)
+    velocity_plane(nx + 1, 0)
+    smooth_plane(nx, 0)
+    hat_plane(nx - 1, 0)
+    sums = line_plane(nx - 3, sums)
+    hat_plane(nx, 0)
+    sums = line_plane(nx - 2, sums)
+    sums = line_plane(nx - 1, sums)
     land(lambda d: d[0] != 0 and d[2] == 0)
 
     def edges(per_side):
         return lambda i: jnp.where(i < len(per_side), per_side[0] + i, nx + 3 - per_side[-1] + i - len(per_side))
     near, inner_planes = edges([1, 2]), edges([2, 3])
-    lax.fori_loop(0, 4, lambda i, c: field_plane(near(i), c), 0)
-    lax.fori_loop(0, 2, lambda i, c: velocity_plane(i * (nx + 3), c), 0)
-    lax.fori_loop(0, 4, lambda i, c: smooth_plane(near(i), c), 0)
-    lax.fori_loop(0, 4, lambda i, c: hat_plane(near(i), c), 0)
-    sums = lax.fori_loop(0, 4, lambda i, c: line_plane(inner_planes(i), c), sums)
+    lax.fori_loop(0, 4, lambda i, c: field_plane(near(i), c), 0, unroll=4)
+    lax.fori_loop(0, 2, lambda i, c: velocity_plane(i * (nx + 3), c), 0, unroll=2)
+    lax.fori_loop(0, 4, lambda i, c: smooth_plane(near(i), c), 0, unroll=4)
+    lax.fori_loop(0, 4, lambda i, c: hat_plane(near(i), c), 0, unroll=4)
+    sums = lax.fori_loop(0, 4, lambda i, c: line_plane(inner_planes(i), c), sums, unroll=4)
     land(lambda d: d[2] != 0)
 
     yr = ny + 8
@@ -493,7 +554,7 @@
     assert nz % 128 == 0 and ny % 8 == 0 and G6 * (nx + 4) <= 128 and nx >= 6
     nt, px, yr = nz // 128, nx + 4, ny + 8
     f32 = jnp.float32
-    copies = len(span_offsets) + 3 * len(plane_offsets)
+    copies = len(span_offsets) + (2 * chunks + 1) * len(plane_offsets)
     dmag, coef = pl.pallas_call(
         functools.partial(kernel, sizes),
         out_shape=(jax.ShapeDtypeStruct((nx, ny, nz), f32), jax.ShapeDtypeStruct((ny, 128), f32)),
@@ -516,6 +577,7 @@
             pltpu.VMEM((NZ, ny, 128), f32),
             pltpu.VMEM((NX * NY, 8, 128), f32),
             pltpu.VMEM((nx, ny, nz), f32),
+            pltpu.VMEM((nz, nz), jnp.bfloat16),
             pltpu.SemaphoreType.DMA((2 * nt + 1,)),
             pltpu.SemaphoreType.DMA((copies,)),
             pltpu.SemaphoreType.DMA((copies,)),

time: 32 us -> 28.5 us (0.89)
  Pallas kernels: 29.5 us -> 26 us
    pallas_call x1, Pallas kernels: 28.7 us -> 25.1 us  [per_device(): pl.pallas_call(functools.partial(kernel, sizes), out_shape=(jax.ShapeDtyp...]
where the time goes in v2:
time: 28.5 us; the launch traced here: 28.2 us
  Pallas kernels  26 us (91%)
  local copies, waits for them, and re-layouts  1.64 us (6%)
  between operations  0.65 us (2%)
    pallas_call x1, Pallas kernels, per_device(): pl.pallas_call(functools.partial(kernel, sizes), out_shape=(jax.ShapeDtyp...  25.1 us
    unnamed x4, local copies, waits for them, and re-layouts  1.64 us
    pallas_call x1, Pallas kernels, per_device(): pl.pallas_call(scale_kernel, out_shape=(jax.ShapeDtypeStruct((nx, ny, nz)...  0.84 us

profile of v2, /device:TPU:0, one launch (start us, length us, event | category | flops | bytes accessed | tf_op | source)
XLA Modules:
  0.0 28.2 jit_solution(10953105828551383697)
XLA Ops:
  0.6 25.1 %shard_map.41 = (f32[16,16,256]{2,1,0:T(8,128)}, f32[16,128]{1,0:T(8,128)}) custom-call(f32[3,16,16,256]{3,2,1,0:T(8,128)} %vel.1, f32[3,16,16,256]{3,2,1,0:T(8,128)} %met.1), custom_call_target="tpu_custom_call" | custom-call | tf_op jit(solution)/shard_map/pallas_call | solution.py:558
  25.8 0.0 copy-start
  25.8 0.9 %copy-done = f32[16,16,256]{2,1,0:T(8,128)S(1)} copy-done((f32[16,16,256]{2,1,0:T(8,128)S(1)}, f32[16,16,256]{2,1,0:T(8,128)}, u32[]{:S(2)}) %copy-start) | copy-done | bytes 262168
  26.7 0.0 copy-start.1
  26.7 0.7 %copy-done.1 = f32[16,128]{1,0:T(8,128)S(1)} copy-done((f32[16,128]{1,0:T(8,128)S(1)}, f32[16,128]{1,0:T(8,128)}, u32[]{:S(2)}) %copy-start.1) | copy-done | bytes 8216
  27.4 0.8 %shard_map.42 = (f32[16,16,256]{2,1,0:T(8,128)}, f32[16,16]{1,0:T(8,128)}) custom-call(f32[16,16,256]{2,1,0:T(8,128)S(1)} %copy-done, f32[16,128]{1,0:T(8,128)S(1)} %copy-done.1), custom_call_target="tpu_custom_call" | custom-call | tf_op jit(solution)/shard_map/pallas_call | solution.py:591
Async XLA Ops:
  25.8 1.0 %copy-start = (f32[16,16,256]{2,1,0:T(8,128)S(1)}, f32[16,16,256]{2,1,0:T(8,128)}, u32[]{:S(2)}) copy-start(f32[16,16,256]{2,1,0:T(8,128)} %get-tuple-element.4.D) | copy-start | bytes 786436
  26.7 0.7 %copy-start.1 = (f32[16,128]{1,0:T(8,128)S(1)}, f32[16,128]{1,0:T(8,128)}, u32[]{:S(2)}) copy-start(f32[16,128]{1,0:T(8,128)} %get-tuple-element.5.coef) | copy-start | bytes 24580

commit v3 on v2

--- a/solution.py
+++ b/solution.py
@@ -43,7 +43,7 @@
     return num * dq, (den + 0.5 * off) * (dq * dq)
 
 
-def kernel(sizes, vel, met, d_out, coef_out, V, Gv, G, H, Q, M, F, TE, E, EF, EG, PK, R, LS, PS, D, W, sem_in, send, recv, lsend, lrecv, psend, precv):
+def kernel(sizes, vel, met, D, coef_out, V, Gv, G, H, Q, M, F, TE, E, EF, EG, PK, R, LS, PS, W, sem_in, send, recv, lsend, lrecv, psend, precv):
     NX, NY, NZ = sizes
     nx, ny, nz = vel.shape[1:]
     nt = nz // 128
@@ -133,18 +133,6 @@
         s = s % 128
         return pltpu.roll(a, s, 1) if s else a
 
-    for f in range(6):
-        for s in range(2):
-            acc = jnp.zeros((ny, 128), jnp.float32)
-            for p in range(2, 2 + nx):
-                tile = V[f, 0 if s == 0 else nt - 1, p, 2 : 2 + ny, :]
-                acc = jnp.where(group == p, lroll(tile, G6 * p - (0 if s == 0 else 122)), acc)
-            TE[s, f, 2 : 2 + ny, :] = acc
-    for s in range(2):
-        for k in range(2):
-            parts = [lroll(TE[s, 3 * k + c, 2 : 2 + ny, :], 2 * c - (0 if s == 0 else 4)) for c in range(3)]
-            PK[s, k] = jnp.where(inner < 2, parts[0], jnp.where(inner < 4, parts[1], parts[2]))
-
     pl.semaphore_wait(barrier, expected)
 
     def span_x(dx, deep):
@@ -187,19 +175,41 @@
                 ys, yd, yn = span_y(dy, k == 0)
                 f0 = 3 * k
                 out.append(remote(V.at[f0 : f0 + 3, :, xs : xs + xn, ys : ys + yn, :], V.at[f0 : f0 + 3, :, xd : xd + xn, yd : yd + yn, :], base + 2 * c + k, d))
-        if dx == 0 and part in (None, chunks - 1):
-            ys, yd, yn = span_y(dy, True)
-            out.append(remote(TE.at[:, :, ys : ys + yn, :], TE.at[:, :, yd : yd + yn, :], base + 2 * chunks, d))
         return out
+
+    def edge_rows(n):
+        dx, dy = plane_offsets[n]
+        ys, yd, yn = span_y(dy, True)
+        return remote(TE.at[:, :, ys : ys + yn, :], TE.at[:, :, yd : yd + yn, :], len(span_offsets) + (2 * chunks + 1) * n + 2 * chunks, (dx, dy, 0))
 
     everything = [(d, (lambda n=n: [span_copy(n)])) for n, d in enumerate(span_offsets)]
     everything += [((dx, dy, 0), (lambda n=n: plane_copies(n))) for n, (dx, dy) in enumerate(plane_offsets)]
-    for d, make in everything:
-        def go(make=make):
-            for c in make():
-                c.start()
-        when(exists(d[0], d[1]), go)
-
+    def send_all(wanted):
+        for d, make in everything:
+            if wanted(d):
+                def go(make=make):
+                    for c in make():
+                        c.start()
+                when(exists(d[0], d[1]), go)
+
+    send_all(lambda d: d[2] == 0 and d[0] == 0)
+    send_all(lambda d: d[2] == 0 and d[0] != 0)
+    for f in range(6):
+        for s in range(2):
+            acc = jnp.zeros((ny, 128), jnp.float32)
+            for p in range(2, 2 + nx):
+                tile = V[f, 0 if s == 0 else nt - 1, p, 2 : 2 + ny, :]
+                acc = jnp.where(group == p, lroll(tile, G6 * p - (0 if s == 0 else 122)), acc)
+            TE[s, f, 2 : 2 + ny, :] = acc
+    for s in range(2):
+        for k in range(2):
+            parts = [lroll(TE[s, 3 * k + c, 2 : 2 + ny, :], 2 * c - (0 if s == 0 else 4)) for c in range(3)]
+            PK[s, k] = jnp.where(inner < 2, parts[0], jnp.where(inner < 4, parts[1], parts[2]))
+
+    for n, (dx, dy) in enumerate(plane_offsets):
+        if dx == 0:
+            when(exists(dx, dy), lambda n=n: edge_rows(n).start())
+    send_all(lambda d: d[2] != 0)
     def land(wanted):
         for d, make in everything:
             if wanted(d):
@@ -376,6 +386,15 @@
             sums = lax.fori_loop(8, hi + 1, step, sums)
         else:
             sums = lax.fori_loop(lo, hi + 1, step, sums)
+    land(lambda d: d[0] != 0 and d[2] == 0)
+
+    land(lambda d: d[2] != 0)
+    for n, (dx, dy) in enumerate(plane_offsets):
+        if dx == 0:
+            when(exists(dx, -dy), lambda n=n: edge_rows(n).wait_recv())
+    def edges(per_side):
+        return lambda i: jnp.where(i < len(per_side), per_side[0] + i, nx + 3 - per_side[-1] + i - len(per_side))
+    near, inner_planes = edges([1, 2]), edges([2, 3])
     velocity_plane(nx + 1, 0)
     smooth_plane(nx, 0)
     hat_plane(nx - 1, 0)
@@ -383,17 +402,11 @@
     hat_plane(nx, 0)
     sums = line_plane(nx - 2, sums)
     sums = line_plane(nx - 1, sums)
-    land(lambda d: d[0] != 0 and d[2] == 0)
-
-    def edges(per_side):
-        return lambda i: jnp.where(i < len(per_side), per_side[0] + i, nx + 3 - per_side[-1] + i - len(per_side))
-    near, inner_planes = edges([1, 2]), edges([2, 3])
     lax.fori_loop(0, 4, lambda i, c: field_plane(near(i), c), 0, unroll=4)
     lax.fori_loop(0, 2, lambda i, c: velocity_plane(i * (nx + 3), c), 0, unroll=2)
     lax.fori_loop(0, 4, lambda i, c: smooth_plane(near(i), c), 0, unroll=4)
     lax.fori_loop(0, 4, lambda i, c: hat_plane(near(i), c), 0, unroll=4)
     sums = lax.fori_loop(0, 4, lambda i, c: line_plane(inner_planes(i), c), sums, unroll=4)
-    land(lambda d: d[2] != 0)
 
     yr = ny + 8
     lane_r = lax.broadcasted_iota(jnp.int32, (yr, 128), 1)
@@ -492,8 +505,6 @@
             if t == nt - 1:
                 tile = jnp.where(lane == 127, lroll(hi_fix, 127 - (G6 * p + 3)), tile)
             D[x, :, 128 * t : 128 * t + 128] = tile
-    save = pltpu.make_async_copy(D, d_out, sem_in.at[2 * nt])
-    save.start()
 
     for o in range(1, NZ):
         line_landing(o).wait_recv()
@@ -525,13 +536,15 @@
             for c in make():
                 c.wait_send()
         when(exists(d[0], d[1]), left)
+    for n, (dx, dy) in enumerate(plane_offsets):
+        if dx == 0:
+            when(exists(dx, dy), lambda n=n: edge_rows(n).wait_send())
     for j, (a, b) in enumerate(plane_peers):
         peak_copy(j, a, b, True).wait_recv()
     peak = PS[0]
     for j in range(1, NX * NY):
         peak = jnp.maximum(peak, PS[j])
     coef_out[...] = jnp.minimum(coef, 0.5 * jnp.max(peak, axis=(0, 1), keepdims=True))
-    save.wait()
     for j, (a, b) in enumerate(plane_peers):
         peak_copy(j, a, b, False).wait_send()
 
@@ -557,9 +570,9 @@
     copies = len(span_offsets) + (2 * chunks + 1) * len(plane_offsets)
     dmag, coef = pl.pallas_call(
         functools.partial(kernel, sizes),
-        out_shape=(jax.ShapeDtypeStruct((nx, ny, nz), f32), jax.ShapeDtypeStruct((ny, 128), f32)),
+        out_shape=(pltpu.VMEM((nx, ny, nz), f32), pltpu.VMEM((ny, 128), f32)),
         in_specs=[pl.BlockSpec(memory_space=pltpu.HBM)] * 2,
-        out_specs=(pl.BlockSpec(memory_space=pltpu.HBM), pl.BlockSpec(memory_space=pltpu.VMEM)),
+        out_specs=(pl.BlockSpec(memory_space=pltpu.VMEM), pl.BlockSpec(memory_space=pltpu.VMEM)),
         scratch_shapes=[
             pltpu.VMEM((6, nt, px, yr, 128), f32),
             pltpu.VMEM((3, nt, px, yr, 128), f32),
@@ -576,7 +589,6 @@
             pltpu.VMEM((2, 3, 2, yr, 128), f32),
             pltpu.VMEM((NZ, ny, 128), f32),
             pltpu.VMEM((NX * NY, 8, 128), f32),
-            pltpu.VMEM((nx, ny, nz), f32),
             pltpu.VMEM((nz, nz), jnp.bfloat16),
             pltpu.SemaphoreType.DMA((2 * nt + 1,)),
             pltpu.SemaphoreType.DMA((copies,)),

time: 28.5 us -> 28 us (0.982)
  local copies, waits for them, and re-layouts: 1.64 us -> 0 us
  Pallas kernels: 26 us -> 27.3 us
    unnamed x4 -> x0, local copies, waits for them, and re-layouts: 1.64 us -> none
    pallas_call x1, Pallas kernels: 25.1 us -> 26.4 us  [per_device(): pl.pallas_call(functools.partial(kernel, sizes), out_shape=(pltpu.VMEM((n...]
where the time goes in v3:
time: 28 us; the launch traced here: 27.9 us
  Pallas kernels  27.3 us (98%)
  between operations  0.64 us (2%)
    pallas_call x1, Pallas kernels, per_device(): pl.pallas_call(functools.partial(kernel, sizes), out_shape=(pltpu.VMEM((n...  26.4 us
    pallas_call x1, Pallas kernels, per_device(): pl.pallas_call(scale_kernel, out_shape=(jax.ShapeDtypeStruct((nx, ny, nz)...  0.84 us

profile of v3, /device:TPU:0, one launch (start us, length us, event | category | flops | bytes accessed | tf_op | source)
XLA Modules:
  0.0 27.9 jit_solution(8713075484821293010)
XLA Ops:
  0.6 26.4 %shard_map.41 = (f32[16,16,256]{2,1,0:T(8,128)S(1)}, f32[16,128]{1,0:T(8,128)S(1)}) custom-call(f32[3,16,16,256]{3,2,1,0:T(8,128)} %vel.1, f32[3,16,16,256]{3,2,1,0:T(8,128)} %met.1), custom_call_target="tpu_custom_call" | custom-call | tf_op jit(solution)/shard_map/pallas_call | solution.py:571
  27.1 0.8 %shard_map.42 = (f32[16,16,256]{2,1,0:T(8,128)}, f32[16,16]{1,0:T(8,128)}) custom-call(f32[16,16,256]{2,1,0:T(8,128)S(1)} %get-tuple-element.4.D, f32[16,128]{1,0:T(8,128)S(1)} %get-tuple-element.5.coef), custom_call_target="tpu_custom_call" | custom-call | tf_op jit(solution)/shard_map/pallas_call | solution.py:603

commit v4 on v3

--- a/solution.py
+++ b/solution.py
@@ -43,7 +43,7 @@
     return num * dq, (den + 0.5 * off) * (dq * dq)
 
 
-def kernel(sizes, vel, met, D, coef_out, V, Gv, G, H, Q, M, F, TE, E, EF, EG, PK, R, LS, PS, W, sem_in, send, recv, lsend, lrecv, psend, precv):
+def kernel(sizes, vel, met, D, coef_out, V, Gv, G, H, Q, M, F, TE, E, EF, EG, PK, R, LS, PS, W, token, sem_in, send, recv, lsend, lrecv, psend, precv):
     NX, NY, NZ = sizes
     nx, ny, nz = vel.shape[1:]
     nt = nz // 128
@@ -81,18 +81,23 @@
 
     barrier = pltpu.get_barrier_semaphore()
     expected = jnp.int32(0)
-    for d in span_offsets + [(dx, dy, 0) for dx, dy in plane_offsets]:
-        ok = exists(d[0], d[1])
-        def sig(d=d):
-            pl.semaphore_signal(barrier, inc=1, device_id=dev(d), device_id_type=MESH)
-        when(ok, sig)
-        expected = expected + (1 if ok is None else ok.astype(jnp.int32))
-    for o in range(1, NZ):
-        pl.semaphore_signal(barrier, inc=1, device_id=(ix, iy, lax.rem(iz + o, NZ)), device_id_type=MESH)
     plane_peers = [(a, b) for a in range(NX) for b in range(NY) if (a, b) != (0, 0)]
     for a, b in plane_peers:
         pl.semaphore_signal(barrier, inc=1, device_id=(lax.rem(ix + a, NX), lax.rem(iy + b, NY), iz), device_id_type=MESH)
-    expected = expected + (NZ - 1 + len(plane_peers))
+    expected = expected + len(plane_peers)
+    for dz in (1, -1):
+        ok = there(dz, iz, NZ)
+        pl.when(ok)(lambda dz=dz: pl.semaphore_signal(barrier, inc=1, device_id=(ix, iy, iz + dz), device_id_type=MESH))
+        expected = expected + ok.astype(jnp.int32)
+
+    def tell(dz):
+        pl.when(there(dz, iz, NZ))(lambda: pl.semaphore_signal(token.at[(dz + 1) // 2], inc=1, device_id=(ix, iy, iz + dz), device_id_type=MESH))
+
+    def relay(dz):
+        def hear():
+            pl.semaphore_wait(token.at[(dz + 1) // 2], 1)
+            tell(dz)
+        pl.when(there(-dz, iz, NZ))(hear)
 
     z2 = jnp.zeros((2, 128), jnp.float32)
     for dx, p0 in ((-1, 0), (1, nx + 2)):
@@ -121,6 +126,9 @@
                         R[s, dxi, k, r0 : r0 + 2, :] = z2
         pl.when(jnp.logical_not(there(dy, iy, NY)))(clear_rows)
 
+    pl.semaphore_wait(barrier, expected)
+    for dz in (1, -1):
+        pl.when(jnp.logical_not(there(-dz, iz, NZ)))(functools.partial(tell, dz))
     for c in loads:
         c.wait()
 
@@ -133,7 +141,6 @@
         s = s % 128
         return pltpu.roll(a, s, 1) if s else a
 
-    pl.semaphore_wait(barrier, expected)
 
     def span_x(dx, deep):
         if dx == 0:
@@ -192,8 +199,15 @@
                         c.start()
                 when(exists(d[0], d[1]), go)
 
-    send_all(lambda d: d[2] == 0 and d[0] == 0)
-    send_all(lambda d: d[2] == 0 and d[0] != 0)
+    def send_chunk(c):
+        for n, (dx, dy) in enumerate(plane_offsets):
+            if dx == 0:
+                def go(n=n):
+                    for cp in plane_copies(n, c):
+                        cp.start()
+                when(exists(0, dy), go)
+
+    send_chunk(0)
     for f in range(6):
         for s in range(2):
             acc = jnp.zeros((ny, 128), jnp.float32)
@@ -206,9 +220,14 @@
             parts = [lroll(TE[s, 3 * k + c, 2 : 2 + ny, :], 2 * c - (0 if s == 0 else 4)) for c in range(3)]
             PK[s, k] = jnp.where(inner < 2, parts[0], jnp.where(inner < 4, parts[1], parts[2]))
 
+    for c in range(1, chunks):
+        send_chunk(c)
     for n, (dx, dy) in enumerate(plane_offsets):
         if dx == 0:
             when(exists(dx, dy), lambda n=n: edge_rows(n).start())
+    send_all(lambda d: d[2] == 0 and d[0] != 0)
+    relay(1)
+    relay(-1)
     send_all(lambda d: d[2] != 0)
     def land(wanted):
         for d, make in everything:
@@ -292,7 +311,7 @@
             s = banded(jnp.concatenate(s, axis=0))
             for k in range(12):
                 for t in range(nt):
-                    G[k, t, x] = s[(k - k0) * ny : (k - k0 + 1) * ny, 128 * t : 128 * t + 128]
+                    G[k, t, x, 0:ny, :] = s[(k - k0) * ny : (k - k0 + 1) * ny, 128 * t : 128 * t + 128]
         return 0
 
     has_lo = jnp.where(iy > 0, 0.125, 0.0)
@@ -362,51 +381,52 @@
                         cp.wait_recv()
                 when(exists(0, -dy), arrive)
 
-    def step(i, sums, smooth=True, hat=True, line=True):
-        if line:
-            sums = line_plane(i - 4, sums)
-        if hat:
-            hat_plane(i - 2, 0)
-        if smooth:
-            smooth_plane(i - 1, 0)
-        field_plane(i, 0)
+    def land_x():
+        land(lambda d: d[0] != 0 and d[2] == 0)
+
+    def order(i):
+        return jnp.where(i < nx, i + 3, nx + 2 - i)
+
+    def line_order(i):
+        return jnp.where(i < nx - 2, i + 4, nx + 1 - i)
+
+    def step(i, sums):
+        for at, wait in waits:
+            pl.when(i == at)(wait)
+        sums = line_plane(line_order(i - 5), sums)
+        hat_plane(order(i - 2), 0)
+        smooth_plane(order(i - 1), 0)
+        field_plane(order(i), 0)
         return sums
 
+    def far_velocity():
+        lax.fori_loop(0, 2, lambda i, c: velocity_plane(i * (nx + 3), c), 0)
+
+    def land_far():
+        land_x()
+        far_velocity()
+
+    need = [0] + [chunk * c - 2 for c in range(1, chunks)]
+    waits = [(at, functools.partial(land_chunk, c)) for c, at in enumerate(need) if at >= 5] + [(nx - 2, land_far)]
     sums = tuple(jnp.zeros((8, 128), jnp.float32) for _ in range(0, ny, 8))
-    for c in range(chunks):
-        land_chunk(c)
-        lo = 3 if c == 0 else chunk * c + 1
-        hi = chunk * (c + 1)
-        if c == 0:
-            velocity_plane(2, 0)
-            step(3, sums, False, False, False)
-            lax.fori_loop(4, hi + 1, lambda i, q: step(i, q, True, False, False), ())
-        elif c == 1:
-            lax.fori_loop(lo, min(hi + 1, 8), lambda i, q: step(i, q, True, True, False), ())
-            sums = lax.fori_loop(8, hi + 1, step, sums)
-        else:
-            sums = lax.fori_loop(lo, hi + 1, step, sums)
-    land(lambda d: d[0] != 0 and d[2] == 0)
-
+    land_chunk(0)
+    velocity_plane(2, 0)
+    def early(i, c):
+        for q, at in enumerate(need):
+            if 0 < at < 5:
+                pl.when(i == at)(functools.partial(land_chunk, q))
+        return field_plane(order(i), c)
+    lax.fori_loop(0, 5, early, 0)
+    lax.fori_loop(0, 4, lambda i, c: smooth_plane(order(i), c), 0)
+    lax.fori_loop(0, 3, lambda i, c: hat_plane(order(i), c), 0)
+    sums = lax.fori_loop(5, nx + 2, step, sums)
+    smooth_plane(order(nx + 1), 0)
+    lax.fori_loop(nx, nx + 2, lambda i, c: hat_plane(order(i), c), 0)
+    sums = lax.fori_loop(nx - 3, nx, lambda i, c: line_plane(line_order(i), c), sums)
     land(lambda d: d[2] != 0)
     for n, (dx, dy) in enumerate(plane_offsets):
         if dx == 0:
             when(exists(dx, -dy), lambda n=n: edge_rows(n).wait_recv())
-    def edges(per_side):
-        return lambda i: jnp.where(i < len(per_side), per_side[0] + i, nx + 3 - per_side[-1] + i - len(per_side))
-    near, inner_planes = edges([1, 2]), edges([2, 3])
-    velocity_plane(nx + 1, 0)
-    smooth_plane(nx, 0)
-    hat_plane(nx - 1, 0)
-    sums = line_plane(nx - 3, sums)
-    hat_plane(nx, 0)
-    sums = line_plane(nx - 2, sums)
-    sums = line_plane(nx - 1, sums)
-    lax.fori_loop(0, 4, lambda i, c: field_plane(near(i), c), 0, unroll=4)
-    lax.fori_loop(0, 2, lambda i, c: velocity_plane(i * (nx + 3), c), 0, unroll=2)
-    lax.fori_loop(0, 4, lambda i, c: smooth_plane(near(i), c), 0, unroll=4)
-    lax.fori_loop(0, 4, lambda i, c: hat_plane(near(i), c), 0, unroll=4)
-    sums = lax.fori_loop(0, 4, lambda i, c: line_plane(inner_planes(i), c), sums, unroll=4)
 
     yr = ny + 8
     lane_r = lax.broadcasted_iota(jnp.int32, (yr, 128), 1)
@@ -496,16 +516,17 @@
         line_copy(o).start()
 
     lo_fix, hi_fix = EF[0, 16, 2 : 2 + ny, :], EF[1, 16, 2 : 2 + ny, :]
-    for x in range(nx):
+    def weight_plane(x, _):
         p = x + 2
         for t in range(nt):
             tile = M[t, p, 2 : 2 + ny, :]
             if t == 0:
-                tile = jnp.where(lane == 0, lroll(lo_fix, -(G6 * p + 2)), tile)
+                tile = jnp.where(lane == 0, pltpu.roll(lo_fix, 126 - G6 * p, 1), tile)
             if t == nt - 1:
-                tile = jnp.where(lane == 127, lroll(hi_fix, 127 - (G6 * p + 3)), tile)
+                tile = jnp.where(lane == 127, pltpu.roll(hi_fix, 124 - G6 * p, 1), tile)
             D[x, :, 128 * t : 128 * t + 128] = tile
-
+        return 0
+    lax.fori_loop(0, nx, weight_plane, 0, unroll=4)
     for o in range(1, NZ):
         line_landing(o).wait_recv()
     total = LS[0]
@@ -565,7 +586,7 @@
     nx, ny, nz = velocity.shape[1:]
     NX, NY, NZ = sizes
     assert nz % 128 == 0 and ny % 8 == 0 and G6 * (nx + 4) <= 128 and nx >= 6
-    nt, px, yr = nz // 128, nx + 4, ny + 8
+    nt, pa, yr = nz // 128, nx + 4 + (nx + 1) % 2, ny + 8
     f32 = jnp.float32
     copies = len(span_offsets) + (2 * chunks + 1) * len(plane_offsets)
     dmag, coef = pl.pallas_call(
@@ -574,13 +595,13 @@
         in_specs=[pl.BlockSpec(memory_space=pltpu.HBM)] * 2,
         out_specs=(pl.BlockSpec(memory_space=pltpu.VMEM), pl.BlockSpec(memory_space=pltpu.VMEM)),
         scratch_shapes=[
-            pltpu.VMEM((6, nt, px, yr, 128), f32),
-            pltpu.VMEM((3, nt, px, yr, 128), f32),
-            pltpu.VMEM((12, nt, px, ny, 128), f32),
-            pltpu.VMEM((3, nt, px, yr, 128), f32),
-            pltpu.VMEM((nt, px, yr, 128), f32),
-            pltpu.VMEM((nt, px, yr, 128), f32),
-            pltpu.VMEM((12, nt, px, yr, 128), f32),
+            pltpu.VMEM((6, nt, pa, yr, 128), f32),
+            pltpu.VMEM((3, nt, pa, yr, 128), f32),
+            pltpu.VMEM((12, nt, pa, yr, 128), f32),
+            pltpu.VMEM((3, nt, pa, yr, 128), f32),
+            pltpu.VMEM((nt, pa, yr, 128), f32),
+            pltpu.VMEM((nt, pa, yr, 128), f32),
+            pltpu.VMEM((12, nt, pa, yr, 128), f32),
             pltpu.VMEM((2, 6, yr, 128), f32),
             pltpu.VMEM((2, 6, yr, 128), f32),
             pltpu.VMEM((2, 17, yr, 128), f32),
@@ -590,6 +611,7 @@
             pltpu.VMEM((NZ, ny, 128), f32),
             pltpu.VMEM((NX * NY, 8, 128), f32),
             pltpu.VMEM((nz, nz), jnp.bfloat16),
+            pltpu.SemaphoreType.REGULAR((2,)),
             pltpu.SemaphoreType.DMA((2 * nt + 1,)),
             pltpu.SemaphoreType.DMA((copies,)),
             pltpu.SemaphoreType.DMA((copies,)),

time: 28 us -> 27.1 us (0.968)
  Pallas kernels: 27.3 us -> 26.3 us
    pallas_call x1, Pallas kernels: 26.4 us -> 25.5 us  [per_device(): pl.pallas_call(functools.partial(kernel, sizes), out_shape=(pltpu.VMEM((n...]
where the time goes in v4:
time: 27.1 us; the launch traced here: 27 us
  Pallas kernels  26.3 us (97%)
  between operations  0.64 us (2%)
    pallas_call x1, Pallas kernels, per_device(): pl.pallas_call(functools.partial(kernel, sizes), out_shape=(pltpu.VMEM((n...  25.5 us
    pallas_call x1, Pallas kernels, per_device(): pl.pallas_call(scale_kernel, out_shape=(jax.ShapeDtypeStruct((nx, ny, nz)...  0.84 us

profile of v4, /device:TPU:0, one launch (start us, length us, event | category | flops | bytes accessed | tf_op | source)
XLA Modules:
  0.0 27.0 jit_solution(3939126018787577014)
XLA Ops:
  0.6 25.5 %shard_map.41 = (f32[16,16,256]{2,1,0:T(8,128)S(1)}, f32[16,128]{1,0:T(8,128)S(1)}) custom-call(f32[3,16,16,256]{3,2,1,0:T(8,128)} %vel.1, f32[3,16,16,256]{3,2,1,0:T(8,128)} %met.1), custom_call_target="tpu_custom_call" | custom-call | tf_op jit(solution)/shard_map/pallas_call | solution.py:592
  26.1 0.8 %shard_map.42 = (f32[16,16,256]{2,1,0:T(8,128)}, f32[16,16]{1,0:T(8,128)}) custom-call(f32[16,16,256]{2,1,0:T(8,128)S(1)} %get-tuple-element.4.D, f32[16,128]{1,0:T(8,128)S(1)} %get-tuple-element.5.coef), custom_call_target="tpu_custom_call" | custom-call | tf_op jit(solution)/shard_map/pallas_call | solution.py:625

commit v5 on v4

--- a/solution.py
+++ b/solution.py
@@ -43,7 +43,7 @@
     return num * dq, (den + 0.5 * off) * (dq * dq)
 
 
-def kernel(sizes, vel, met, D, coef_out, V, Gv, G, H, Q, M, F, TE, E, EF, EG, PK, R, LS, PS, W, token, sem_in, send, recv, lsend, lrecv, psend, precv):
+def kernel(sizes, vel, met, D, coef_out, V, Gv, G, H, Q, M, F, TE, E, EF, EG, PK, R, LS, PS, W, W2, token, sem_in, send, recv, lsend, lrecv, psend, precv):
     NX, NY, NZ = sizes
     nx, ny, nz = vel.shape[1:]
     nt = nz // 128
@@ -289,8 +289,10 @@
     gap = jnp.abs(zi - zj)
     W[...] = jnp.where(gap == 0, 2.0, jnp.where((gap == 1) | (gap == nz - 1), 1.0, 0.0)).astype(jnp.bfloat16)
 
-    def banded(a):
-        w = W[...]
+    gap = jnp.abs(zi[0:128, 0:128] - zj[0:128, 0:128])
+    W2[...] = jnp.where(gap == 0, 4.0, jnp.where((gap == 1) | (gap == G6), 2.0, jnp.where((gap == G6 - 1) | (gap == G6 + 1), 1.0, 0.0))).astype(jnp.bfloat16)
+
+    def banded(a, w):
         hi = a.astype(jnp.bfloat16)
         rest = a - hi.astype(jnp.float32)
         mid = rest.astype(jnp.bfloat16)
@@ -308,7 +310,7 @@
                     mid = F[k, t, x, 2 : 2 + ny, :]
                     row.append((mid + mid) + (F[k, t, x, 1 : 1 + ny, :] + F[k, t, x, 3 : 3 + ny, :]))
                 s.append(jnp.concatenate(row, axis=1))
-            s = banded(jnp.concatenate(s, axis=0))
+            s = banded(jnp.concatenate(s, axis=0), W[...])
             for k in range(12):
                 for t in range(nt):
                     G[k, t, x, 0:ny, :] = s[(k - k0) * ny : (k - k0 + 1) * ny, 128 * t : 128 * t + 128]
@@ -385,44 +387,37 @@
         land(lambda d: d[0] != 0 and d[2] == 0)
 
     def order(i):
+        i = jnp.clip(i, 0, nx + 1)
         return jnp.where(i < nx, i + 3, nx + 2 - i)
 
     def line_order(i):
+        i = jnp.clip(i, 0, nx - 1)
         return jnp.where(i < nx - 2, i + 4, nx + 1 - i)
 
     def step(i, sums):
-        for at, wait in waits:
-            pl.when(i == at)(wait)
         sums = line_plane(line_order(i - 5), sums)
         hat_plane(order(i - 2), 0)
         smooth_plane(order(i - 1), 0)
         field_plane(order(i), 0)
         return sums
 
-    def far_velocity():
-        lax.fori_loop(0, 2, lambda i, c: velocity_plane(i * (nx + 3), c), 0)
-
     def land_far():
         land_x()
-        far_velocity()
-
-    need = [0] + [chunk * c - 2 for c in range(1, chunks)]
-    waits = [(at, functools.partial(land_chunk, c)) for c, at in enumerate(need) if at >= 5] + [(nx - 2, land_far)]
+        for p in (0, nx + 3):
+            velocity_plane(p, 0)
+
+    waits = [(chunk * c - 2, functools.partial(land_chunk, c)) for c in range(1, chunks)] + [(nx - 2, land_far)]
     sums = tuple(jnp.zeros((8, 128), jnp.float32) for _ in range(0, ny, 8))
+
+    def turn(j, sums):
+        def arrivals():
+            for at, wait in waits:
+                pl.when(j == at)(wait)
+        pl.when(lax.rem(j + 2, chunk) == 0)(arrivals)
+        return step(j, sums)
     land_chunk(0)
     velocity_plane(2, 0)
-    def early(i, c):
-        for q, at in enumerate(need):
-            if 0 < at < 5:
-                pl.when(i == at)(functools.partial(land_chunk, q))
-        return field_plane(order(i), c)
-    lax.fori_loop(0, 5, early, 0)
-    lax.fori_loop(0, 4, lambda i, c: smooth_plane(order(i), c), 0)
-    lax.fori_loop(0, 3, lambda i, c: hat_plane(order(i), c), 0)
-    sums = lax.fori_loop(5, nx + 2, step, sums)
-    smooth_plane(order(nx + 1), 0)
-    lax.fori_loop(nx, nx + 2, lambda i, c: hat_plane(order(i), c), 0)
-    sums = lax.fori_loop(nx - 3, nx, lambda i, c: line_plane(line_order(i), c), sums)
+    sums = lax.fori_loop(0, nx + 5, turn, sums)
     land(lambda d: d[2] != 0)
     for n, (dx, dy) in enumerate(plane_offsets):
         if dx == 0:
@@ -476,17 +471,17 @@
         for k, (a, b) in enumerate(pairs):
             EF[s, k] = u[a] * u[b]
             EF[s, 6 + k] = mag * f[k]
-        def lanes_smooth(a):
-            b = (a + a) + (shift(a, G6) + shift(a, -G6))
-            return (b + b) + (shift(b, 1) + shift(b, -1))
+        rows = []
         for c in range(3):
-            y = (u[c] + u[c]) + (pltpu.roll(u[c], yr - 1, 0) + pltpu.roll(u[c], 1, 0))
-            EG[s, c] = lanes_smooth(y) * scale_r
+            rows.append((u[c] + u[c]) + (pltpu.roll(u[c], yr - 1, 0) + pltpu.roll(u[c], 1, 0)))
         own = slice(2, 2 + ny)
-        filtered = []
         for k in range(12):
             mid = EF[s, k, own, :]
-            filtered.append(lanes_smooth((mid + mid) + (EF[s, k, 1 : 1 + ny, :] + EF[s, k, 3 : 3 + ny, :])))
+            rows.append((mid + mid) + (EF[s, k, 1 : 1 + ny, :] + EF[s, k, 3 : 3 + ny, :]))
+        smoothed = banded(jnp.concatenate(rows, axis=0), W2[...])
+        for c in range(3):
+            EG[s, c] = smoothed[yr * c : yr * (c + 1)] * scale_r
+        filtered = [smoothed[3 * yr + ny * k : 3 * yr + ny * (k + 1)] for k in range(12)]
         hat, dh = [], [[None] * 3 for _ in range(3)]
         me = [E[s, 3 + c, own, :] for c in range(3)]
         for i in range(3):
@@ -611,6 +606,7 @@
             pltpu.VMEM((NZ, ny, 128), f32),
             pltpu.VMEM((NX * NY, 8, 128), f32),
             pltpu.VMEM((nz, nz), jnp.bfloat16),
+            pltpu.VMEM((128, 128), jnp.bfloat16),
             pltpu.SemaphoreType.REGULAR((2,)),
             pltpu.SemaphoreType.DMA((2 * nt + 1,)),
             pltpu.SemaphoreType.DMA((copies,)),

time: 27.1 us -> 26.4 us (0.974)
  Pallas kernels: 26.3 us -> 25.7 us
    pallas_call x1, Pallas kernels: 25.5 us -> 24.8 us  [per_device(): pl.pallas_call(functools.partial(kernel, sizes), out_shape=(pltpu.VMEM((n...]
where the time goes in v5:
time: 26.4 us; the launch traced here: 26.3 us
  Pallas kernels  25.7 us (97%)
  between operations  0.64 us (2%)
    pallas_call x1, Pallas kernels, per_device(): pl.pallas_call(functools.partial(kernel, sizes), out_shape=(pltpu.VMEM((n...  24.8 us
    pallas_call x1, Pallas kernels, per_device(): pl.pallas_call(scale_kernel, out_shape=(jax.ShapeDtypeStruct((nx, ny, nz)...  0.84 us

profile of v5, /device:TPU:0, one launch (start us, length us, event | category | flops | bytes accessed | tf_op | source)
XLA Modules:
  0.0 26.3 jit_solution(2584858213393716806)
XLA Ops:
  0.6 24.8 %shard_map.41 = (f32[16,16,256]{2,1,0:T(8,128)S(1)}, f32[16,128]{1,0:T(8,128)S(1)}) custom-call(f32[3,16,16,256]{3,2,1,0:T(8,128)} %vel.1, f32[3,16,16,256]{3,2,1,0:T(8,128)} %met.1), custom_call_target="tpu_custom_call" | custom-call | tf_op jit(solution)/shard_map/pallas_call | solution.py:587
  25.4 0.8 %shard_map.42 = (f32[16,16,256]{2,1,0:T(8,128)}, f32[16,16]{1,0:T(8,128)}) custom-call(f32[16,16,256]{2,1,0:T(8,128)S(1)} %get-tuple-element.4.D, f32[16,128]{1,0:T(8,128)S(1)} %get-tuple-element.5.coef), custom_call_target="tpu_custom_call" | custom-call | tf_op jit(solution)/shard_map/pallas_call | solution.py:621

commit v6 on v5

--- a/solution.py
+++ b/solution.py
@@ -43,7 +43,7 @@
     return num * dq, (den + 0.5 * off) * (dq * dq)
 
 
-def kernel(sizes, vel, met, D, coef_out, V, Gv, G, H, Q, M, F, TE, E, EF, EG, PK, R, LS, PS, W, W2, token, sem_in, send, recv, lsend, lrecv, psend, precv):
+def kernel(sizes, vel, met, D, cols, turned, half, V, Gv, G, H, Q, M, F, TE, E, EF, EG, PK, R, LS, PS, W, W2, token, sem_in, send, recv, lsend, lrecv, psend, precv):
     NX, NY, NZ = sizes
     nx, ny, nz = vel.shape[1:]
     nt = nz // 128
@@ -51,14 +51,18 @@
     starts = list(range(1, ny - 6, 8)) + [ny - 5]
     ix, iy, iz = lax.axis_index("gx"), lax.axis_index("gy"), lax.axis_index("gz")
 
+    chunk = nx // chunks
     loads = []
-    for k, src in enumerate((vel, met)):
-        for t in range(nt):
-            loads.append(pltpu.make_async_copy(
-                src.at[:, :, :, 128 * t : 128 * t + 128],
-                V.at[3 * k : 3 * k + 3, t, 2 : 2 + nx, 2 : 2 + ny, :],
-                sem_in.at[k * nt + t]))
-    for c in loads:
+    for x0, x1 in ((0, chunk), (chunk, nx)):
+        part = []
+        for k, src in enumerate((vel, met)):
+            for t in range(nt):
+                part.append(pltpu.make_async_copy(
+                    src.at[:, x0:x1, :, 128 * t : 128 * t + 128],
+                    V.at[3 * k : 3 * k + 3, t, 2 + x0 : 2 + x1, 2 : 2 + ny, :],
+                    sem_in.at[len(loads) * 2 * nt + len(part)]))
+        loads.append(part)
+    for c in loads[0] + loads[1]:
         c.start()
 
     def there(delta, i, n):
@@ -129,7 +133,7 @@
     pl.semaphore_wait(barrier, expected)
     for dz in (1, -1):
         pl.when(jnp.logical_not(there(-dz, iz, NZ)))(functools.partial(tell, dz))
-    for c in loads:
+    for c in loads[0]:
         c.wait()
 
     lane = lax.broadcasted_iota(jnp.int32, (ny, 128), 1)
@@ -164,8 +168,6 @@
         s = 1 if dz == 1 else 0
         ys, yd, yn = span_y(dy, True)
         return remote(PK.at[s, :, ys - 2 : ys - 2 + yn, :], R.at[s, 1 - dx, :, yd : yd + yn, :], n, d)
-
-    chunk = nx // chunks
 
     def plane_copies(n, part=None):
         dx, dy = plane_offsets[n]
@@ -208,6 +210,8 @@
                 when(exists(0, dy), go)
 
     send_chunk(0)
+    for c in loads[1]:
+        c.wait()
     for f in range(6):
         for s in range(2):
             acc = jnp.zeros((ny, 128), jnp.float32)
@@ -545,6 +549,11 @@
             device_id=(tx, ty, iz), device_id_type=MESH)
     for j, (a, b) in enumerate(plane_peers):
         peak_copy(j, a, b, False).start()
+    table = coef.T
+    for x in range(nx):
+        at = G6 * (x + 2) + 2
+        cols[x] = jnp.broadcast_to(jnp.sum(jnp.where(lane == at, coef, 0.0), axis=1, keepdims=True), (ny, 128))
+        turned[x : x + 1, :] = table[at : at + 1, :]
     for o in range(1, NZ):
         line_copy(o).wait_send()
     for d, make in everything:
@@ -560,21 +569,19 @@
     peak = PS[0]
     for j in range(1, NX * NY):
         peak = jnp.maximum(peak, PS[j])
-    coef_out[...] = jnp.minimum(coef, 0.5 * jnp.max(peak, axis=(0, 1), keepdims=True))
+    half[...] = jnp.broadcast_to(0.5 * jnp.max(peak, axis=(0, 1), keepdims=True), (8, 128))
     for j, (a, b) in enumerate(plane_peers):
         peak_copy(j, a, b, False).wait_send()
 
 
-def scale_kernel(D, coef, visc, coef_out):
-    nx, ny = visc.shape[:2]
-    lane = lax.broadcasted_iota(jnp.int32, (ny, 128), 1)
-    table = coef[...]
-    turned = table.T
+def scale_kernel(D, cols, turned, half, visc, coef_out):
+    nx, ny, nz = visc.shape
+    limit = half[0:1, :]
     for x in range(nx):
-        at = G6 * (x + 2) + 2
-        column = jnp.sum(jnp.where(lane == at, table, 0.0), axis=1, keepdims=True)
-        visc[x] = D[x] * column
-        coef_out[x : x + 1, :] = turned[at : at + 1, :]
+        column = jnp.minimum(cols[x], limit)
+        for t in range(0, nz, 128):
+            visc[x, :, t : t + 128] = D[x, :, t : t + 128] * column
+    coef_out[...] = jnp.minimum(turned[...], limit[:, 0:ny])
 
 
 def per_device(sizes, velocity, metric):
@@ -584,11 +591,11 @@
     nt, pa, yr = nz // 128, nx + 4 + (nx + 1) % 2, ny + 8
     f32 = jnp.float32
     copies = len(span_offsets) + (2 * chunks + 1) * len(plane_offsets)
-    dmag, coef = pl.pallas_call(
+    parts = pl.pallas_call(
         functools.partial(kernel, sizes),
-        out_shape=(pltpu.VMEM((nx, ny, nz), f32), pltpu.VMEM((ny, 128), f32)),
+        out_shape=(pltpu.VMEM((nx, ny, nz), f32), pltpu.VMEM((nx, ny, 128), f32), pltpu.VMEM((nx, ny), f32), pltpu.VMEM((8, 128), f32)),
         in_specs=[pl.BlockSpec(memory_space=pltpu.HBM)] * 2,
-        out_specs=(pl.BlockSpec(memory_space=pltpu.VMEM), pl.BlockSpec(memory_space=pltpu.VMEM)),
+        out_specs=(pl.BlockSpec(memory_space=pltpu.VMEM),) * 4,
         scratch_shapes=[
             pltpu.VMEM((6, nt, pa, yr, 128), f32),
             pltpu.VMEM((3, nt, pa, yr, 128), f32),
@@ -608,7 +615,7 @@
             pltpu.VMEM((nz, nz), jnp.bfloat16),
             pltpu.VMEM((128, 128), jnp.bfloat16),
             pltpu.SemaphoreType.REGULAR((2,)),
-            pltpu.SemaphoreType.DMA((2 * nt + 1,)),
+            pltpu.SemaphoreType.DMA((4 * nt,)),
             pltpu.SemaphoreType.DMA((copies,)),
             pltpu.SemaphoreType.DMA((copies,)),
             pltpu.SemaphoreType.DMA((NZ,)),
@@ -616,15 +623,15 @@
             pltpu.SemaphoreType.DMA((NX * NY,)),
             pltpu.SemaphoreType.DMA((NX * NY,)),
         ],
-        compiler_params=pltpu.CompilerParams(collective_id=0, has_side_effects=True, vmem_limit_bytes=67043328 - 600 * 1024),
+        compiler_params=pltpu.CompilerParams(collective_id=0, has_side_effects=True, vmem_limit_bytes=67043328 - 700 * 1024),
     )(velocity, metric)
     return pl.pallas_call(
         scale_kernel,
         out_shape=(jax.ShapeDtypeStruct((nx, ny, nz), f32), jax.ShapeDtypeStruct((nx, ny), f32)),
-        in_specs=[pl.BlockSpec(memory_space=pltpu.VMEM)] * 2,
+        in_specs=[pl.BlockSpec(memory_space=pltpu.VMEM)] * 4,
         out_specs=(pl.BlockSpec(memory_space=pltpu.VMEM),) * 2,
         compiler_params=pltpu.CompilerParams(vmem_limit_bytes=4 * 1024 * 1024),
-    )(dmag, coef)
+    )(*parts)
 
 
 def solution(mesh):

time: 26.4 us -> 26.4 us (level)
  no operation moved by 1% of the time
where the time goes in v6:
time: 26.4 us; the launch traced here: 26.2 us
  Pallas kernels  25.6 us (97%)
  between operations  0.64 us (2%)
    pallas_call x1, Pallas kernels, per_device(): pl.pallas_call(functools.partial(kernel, sizes), out_shape=(pltpu.VMEM((n...  24.9 us
    pallas_call x1, Pallas kernels, per_device(): pl.pallas_call(scale_kernel, out_shape=(jax.ShapeDtypeStruct((nx, ny, nz)...  0.73 us

profile of v6, /device:TPU:0, one launch (start us, length us, event | category | flops | bytes accessed | tf_op | source)
XLA Modules:
  0.0 26.2 jit_solution(6150184378869292250)
XLA Ops:
  0.6 24.9 %shard_map.41 = (f32[16,16,256]{2,1,0:T(8,128)S(1)}, f32[16,16,128]{2,1,0:T(8,128)S(1)}, f32[16,16]{1,0:T(8,128)S(1)}, f32[8,128]{1,0:T(8,128)S(1)}) custom-call(f32[3,16,16,256]{3,2,1,0:T(8,128)} %vel.1, f32[3,16,16,256]{3,2,1,0:T(8,128)} %met.1), custom_call_target="tpu_custom_call" | custom-call | tf_op jit(solution)/shard_map/pallas_call | solution.py:594
  25.5 0.7 %shard_map.42 = (f32[16,16,256]{2,1,0:T(8,128)}, f32[16,16]{1,0:T(8,128)}) custom-call(f32[16,16,256]{2,1,0:T(8,128)S(1)} %get-tuple-element.6.D, f32[16,16,128]{2,1,0:T(8,128)S(1)} %get-tuple-element.7.cols, f32[16,16]{1,0:T(8,128)S(1)} %get-tuple-element.8.turned, f32[8,128]{1,0:T(8,128)S(1)} %get-tuple-element.9.half), custom_call_target="tpu_custom_call" | custom-call | tf_op jit(solution)/shard_map/pallas_call | solution.py:628
